TPU v7x, 256 devices: a 2x2x32 block of a 4x8x32 slice. The times are simulated.
256 devices in a mesh: groups: 4 (over y, x), asset: 64 (over z, core).
Axes of the slice: x: 2, y: 2, z: 32, core: 2. Of those that a mesh axis runs over, the one named last changes fastest.
The devices are a block of a 4x8x32 slice.
Arguments:
- scen_draws: bfloat16 [16384, 256], P(('groups', 'asset')), parts along dimension 0, may hold values from -4 to 4
- factor_mix: bfloat16 [256, 256], replicated, may hold values from -0.375 to 0.375
- loadings: bfloat16 [262144, 256], P(('groups', 'asset')), parts along dimension 0, may hold values from -0.375 to 0.375
- convexity: float32 [262144], P(('groups', 'asset')), parts along dimension 0, may hold values from -0.6 to 0.6
- holdings: float32 [262144], P(('groups', 'asset')), parts along dimension 0, may hold values from -0.110485435 to 0.110485435
- desk_map: int32 [262144], P(('groups', 'asset')), parts along dimension 0, may hold values from 0 to 127
- ranks: int32 [16384], P('groups'), parts along dimension 0, may hold values from 0 to 4095, each once
- desk_prices: float32 [512], P('groups'), parts along dimension 0, may hold values from -5 to 5
Outputs:
- allocation: float32 [512], P('groups'), parts along dimension 0
- grad_loadings: float32 [262144, 256], P(('groups', 'asset')), parts along dimension 0
- grad_convexity: float32 [262144], P(('groups', 'asset')), parts along dimension 0
There are 4 independent parts, one for each index of `groups`. A program takes and returns all parts, laid end to end along the dimension named above; an argument that names none is the same for every part. Nothing has to cross between parts.
All inputs are finite; a program needn't handle non-finite values.
Results may differ from a plain program's by a relative error of at most 0.0029.
Values may be sent and summed in bfloat16 or wider, within the bound.
No kernel may reach another device: no remote copies, remote signals or barrier semaphores. Data moves between devices by JAX's collectives and lax.ppermute only.
A program may use at most 64 MiB of HBM per device.

v0:
```python
import math

import jax
import jax.numpy as jnp
from jax import lax
from jax.sharding import Mesh
from jax.sharding import PartitionSpec as P

DESKS = 128
BAND = 32
CENTER = 166
ASSET = ("asset_0", "asset_1")
GROUPS_ASSET = ("groups", "asset_0", "asset_1")


def filled_up(lines, size):
    spare = -lines.shape[0] % size
    if not spare:
        return lines
    return jnp.concatenate([lines, jnp.zeros((spare, *lines.shape[1:]), lines.dtype)])


def copy_for_each(x, axis):
    copies = jnp.broadcast_to(x, (lax.axis_size(axis), *x.shape))
    return lax.all_to_all(copies, axis, split_axis=0, concat_axis=0, tiled=True)


def laid_out(tiles, dim):
    tiles = jnp.moveaxis(tiles, 0, dim)
    shape = tiles.shape
    return tiles.reshape(*shape[:dim], shape[dim] * shape[dim + 1], *shape[dim + 2 :])


def collect(x, axis, dim):
    tiles = copy_for_each(x, axis)
    return laid_out(tiles, dim)


def cut_along(x, dim, size):
    before, after = (x.shape[:dim], x.shape[dim + 1 :])
    return jnp.moveaxis(x.reshape(*before, size, -1, *after), dim, 0)


def summed_on_arrival(x, axis, dim):
    size = lax.axis_size(axis)
    tiles = lax.all_to_all(cut_along(x, dim, size), axis, 0, 0, tiled=True)
    return jnp.sum(tiles, axis=0)


def total_of(x, axes):
    padded = filled_up(x, lax.axis_size(axes))
    whole = collect(summed_on_arrival(padded, axes, 0), axes, 0)
    return lax.slice_in_dim(whole, 0, len(x)).reshape(x.shape)


def packed_total(arrays, axis):
    ends = [0]
    for a in arrays:
        ends.append(ends[-1] + a.size)
    running = total_of(jnp.concatenate([a.ravel() for a in arrays]), axis)
    return tuple((running[b:e].reshape(a.shape) for a, b, e in zip(arrays, ends, ends[1:])))


def over_axes(x, axes):
    for axis in axes:
        x = lax.psum(x, axis)
    return x


def gather_axes(x, axes, dim):
    far, near = axes
    first = copy_for_each(x, far)
    tiles = jnp.swapaxes(copy_for_each(first, near), 0, 1)
    return laid_out(tiles.reshape(-1, *x.shape), dim)


def smooth_bend(value):
    return jnp.logaddexp(value, -value) - math.log(2.0)


def rank_kernel(ranks, scenarios):
    centre = jnp.float32(CENTER)
    spread = jnp.float32(BAND)
    offsets = (ranks.astype(jnp.float32) - centre) / spread
    every = (jnp.arange(scenarios, dtype=jnp.float32) - centre) / spread
    return jnp.exp(-0.5 * offsets * offsets) / jnp.sum(jnp.exp(-0.5 * every * every))


def cotangent_of(
    weights,
    weight_total,
    slopes,
    smoothing,
    kernel,
    grad_quant,
    grad_band,
    centred,
    prices,
    scenarios,
):
    grad_loss = (
        slopes / smoothing
        + kernel * grad_quant
        + grad_band * 0.09 * centred / (scenarios * smoothing)
    )
    return (
        scenarios * (-weights[:, None] * prices[None, :] / weight_total - grad_loss[:, None])
    ).astype(jnp.bfloat16)


def tail_core(losses, valued, ranks, prices):
    scenarios = losses.shape[0]
    kernel = rank_kernel(ranks, scenarios)
    quantile = jnp.sum(kernel * losses)
    average = jnp.mean(losses)
    centred = losses - average
    smoothing = 0.3 * jnp.sqrt(jnp.mean(centred * centred) + 1e-06)
    scores = (losses - quantile) / smoothing
    weights = jax.nn.sigmoid(scores)
    weight_total = jnp.sum(weights)
    objective = -jnp.sum(weights * valued) / weight_total
    slopes = (-valued - objective) / weight_total * weights * (1.0 - weights)
    grad_quant = -jnp.sum(slopes) / smoothing
    grad_band = -jnp.sum(slopes * scores) / smoothing
    cotangent = cotangent_of(
        weights,
        weight_total,
        slopes,
        smoothing,
        kernel,
        grad_quant,
        grad_band,
        centred,
        prices,
        scenarios,
    )
    return (cotangent, weights, weight_total)


def tail_columns(partial_value, ranks, prices):
    sums = packed_total(
        (-jnp.sum(partial_value, axis=1), jnp.sum(partial_value * prices[None, :], axis=1)), ASSET
    )
    cotangent, weights, weight_total = tail_core(sums[0], sums[1], ranks, prices)
    weighted = over_axes(jnp.sum(weights[:, None] * partial_value, axis=0), ASSET)
    return (cotangent, -weighted / weight_total)


def desk_table(desk_map):
    columns = jnp.arange(DESKS, dtype=jnp.int32)
    return (desk_map[:, None] == columns[None, :]).astype(jnp.bfloat16)


def split_rows(array, block_rows):
    return array.reshape((-1, block_rows) + array.shape[1:])


def exposure_of(shock_rows, loadings):
    return lax.dot_general(
        shock_rows, loadings, (((1,), (1,)), ((), ())), preferred_element_type=jnp.float32
    )


def pnl_rows(shock_rows, loadings, convexity, holdings, table):
    number = shock_rows.shape[0]
    block_rows = math.gcd(number, 512)

    def pnl_one_block(shock_block):
        exposure = exposure_of(shock_block, loadings)
        held = (holdings * (exposure + convexity * smooth_bend(exposure))).astype(jnp.bfloat16)
        return jnp.dot(held, table, preferred_element_type=jnp.float32)

    result = lax.map(pnl_one_block, split_rows(shock_rows, block_rows))
    return result.reshape((number, table.shape[1]))


def grad_rows(carry, shock_rows, cot_rows, loadings, convexity, holdings, table):
    number = shock_rows.shape[0]
    block_rows = math.gcd(number, 512)

    def grad_one_block(state, inputs):
        shock_block, cot_block = inputs
        exposure = exposure_of(shock_block, loadings)
        spread_back = lax.dot_general(
            cot_block, table, (((1,), (1,)), ((), ())), preferred_element_type=jnp.float32
        )
        held = holdings * spread_back
        grad_exposure = (held * (1.0 + convexity * jnp.tanh(exposure))).astype(jnp.bfloat16)
        grad_load = state[0] + lax.dot_general(
            grad_exposure, shock_block, (((0,), (0,)), ((), ())), preferred_element_type=jnp.float32
        )
        grad_conv = state[1] + jnp.sum(held * smooth_bend(exposure), axis=0)
        return ((grad_load, grad_conv), None)

    final, ignored = lax.scan(
        grad_one_block,
        carry,
        (split_rows(shock_rows, block_rows), split_rows(cot_rows, block_rows)),
    )
    return final


def shards(scen_draws, factor_mix, loadings, convexity, holdings, desk_map, ranks, desk_prices):
    local_shocks = jnp.dot(scen_draws, factor_mix, preferred_element_type=jnp.float32).astype(
        jnp.bfloat16
    )
    table = desk_table(desk_map)
    shocks = gather_axes(local_shocks, ("asset_0", "asset_1"), 0)
    partial_value = pnl_rows(shocks, loadings, convexity, holdings, table)
    cotangent, allocation = tail_columns(partial_value, ranks, desk_prices)
    initial = (
        jnp.zeros((loadings.shape[0], loadings.shape[1]), jnp.float32),
        jnp.zeros((loadings.shape[0],), jnp.float32),
    )
    grad_load, grad_conv = grad_rows(
        initial, shocks, cotangent, loadings, convexity, holdings, table
    )
    squares = over_axes(jnp.sum(grad_load * grad_load) + jnp.sum(grad_conv * grad_conv), ASSET)
    entries = loadings.shape[0] * lax.axis_size(ASSET) * (loadings.shape[1] + 1)
    factor = lax.rsqrt(squares / entries + 1e-06)
    return (allocation, grad_load * factor, grad_conv * factor)


def solution(mesh):
    torus = Mesh(
        mesh.devices.reshape(mesh.shape["groups"], 32, 2), ("groups", "asset_0", "asset_1")
    )
    return jax.shard_map(
        shards,
        mesh=torus,
        in_specs=(
            P(GROUPS_ASSET, None),
            P(),
            P(GROUPS_ASSET, None),
            P(GROUPS_ASSET),
            P(GROUPS_ASSET),
            P(GROUPS_ASSET),
            P("groups"),
            P("groups"),
        ),
        out_specs=(P("groups"), P(GROUPS_ASSET, None), P(GROUPS_ASSET)),
        check_vma=False,
    )
```

profile of v0, /device:TPU:38, one launch (start us, length us, event | category | flops | bytes accessed | tf_op | source)
XLA Modules:
  0.0 358.3 jit_solution(15060804531510212304)
XLA Ops:
  3.5 32.7 %all-to-all-start = ((bf16[32,64,256]{2,1,0:T(8,128)(2,1)}), bf16[32,64,256]{2,1,0:T(8,128)(2,1)S(1)}, u32[]{:S(2)}, u32[]{:S(2)}) async-start(bf16[32,64,256]{2,1,0:T(8,128)(2,1)} %broadcast_in_dim.37), calls=%async_computation | async-start | bytes 2097152 | tf_op jit(solution)/shard_map/all_to_all | solution.py:25
  36.2 104.5 %all-to-all-done = bf16[32,64,256]{2,1,0:T(8,128)(2,1)S(1)} async-done(((bf16[32,64,256]{2,1,0:T(8,128)(2,1)}), bf16[32,64,256]{2,1,0:T(8,128)(2,1)S(1)}, u32[]{:S(2)}, u32[]{:S(2)}) %all-to-all-start) | async-done | bytes 1048608 | tf_op jit(solution)/shard_map/all_to_all | solution.py:25
  140.9 5.4 %all_to_all.25 = bf16[2,32,64,256]{3,2,1,0:T(8,128)(2,1)S(1)} all-to-all(bf16[2,32,64,256]{3,2,1,0:T(8,128)(2,1)S(1)} %broadcast_in_dim.38), channel_id=1, replica_groups=mesh['groups'=4,'asset_0'=32,'asset_1'=2] {'asset_1'}, dimensions={0} | all-to-all | bytes 4194304 | tf_op jit(solution)/shard_map/all_to_all | solution.py:25
  147.9 23.4 %while.28 = (s32[]{:T(128)}, f32[8,512,128]{2,1,0:T(8,128)S(1)}, f32[1024]{0:T(1024)S(1)}, bf16[8,512,256]{2,1,0:T(8,128)(2,1)}, bf16[1024,256]{1,0:T(8,128)(2,1...) while((s32[]{:T(128)}, f32[8,512,128]{2,1,0:T(8,128)S(1)}, f32[1024]{0:T(1024)S(1)}, ...), condition=%wide.region_1.2_spmd.clone, body=%wide.region_0.1_spmd.clone.sunk | while | flops 410255360 | bytes 1061981 | solution.py:173
  147.9 2.9 fusion.83
  150.8 2.9 fusion.83
  153.8 2.9 fusion.83
  156.7 2.9 fusion.83
  159.6 2.9 fusion.83
  162.5 2.9 fusion.83
  165.5 2.9 fusion.83
  168.4 2.9 fusion.83
  172.5 31.5 %all_to_all.26 = f32[64,1,128]{2,1,0:T(1,128)S(1)} all-to-all(f32[64,1,128]{2,1,0:T(1,128)S(1)} %bitcast.91), channel_id=1, replica_groups=mesh['groups'=4,'asset_0'=32,'asset_1'=2] {'asset_0','asset_1'}, dimensions={0} | all-to-all | bytes 65536 | tf_op jit(solution)/shard_map/all_to_all | solution.py:46
  204.7 6.6 %all-to-all-start.3 = ((f32[64,1,128]{2,1,0:T(1,128)}), f32[64,1,128]{2,1,0:T(1,128)S(1)}, u32[]{:S(2)}, u32[]{:S(2)}) async-start(f32[64,1,128]{2,1,0:T(1,128)} %broadcast_in_dim.39), calls=%async_computation.3 | async-start | bytes 65536 | tf_op jit(solution)/shard_map/all_to_all | solution.py:25
  212.0 21.1 %all-to-all-done.3 = f32[64,1,128]{2,1,0:T(1,128)S(1)} async-done(((f32[64,1,128]{2,1,0:T(1,128)}), f32[64,1,128]{2,1,0:T(1,128)S(1)}, u32[]{:S(2)}, u32[]{:S(2)}) %all-to-all-start.3) | async-done | bytes 32800 | tf_op jit(solution)/shard_map/all_to_all | solution.py:25
  248.0 47.0 %while.29 = (s32[]{:T(128)}, f32[1024,256]{1,0:T(8,128)S(1)}, f32[1024]{0:T(1024)S(1)}, f32[1024]{0:T(1024)S(1)}, bf16[8,512,128]{2,1,0:T(8,128)(2,1)S(1)}, /*in...) while((s32[]{:T(128)}, f32[1024,256]{1,0:T(8,128)S(1)}, ...), condition=%wide.region_18.19_spmd.clone, body=%wide.region_16.18_spmd.clone.sunk | while | flops 681313280 | bytes 15892648 | solution.py:195
  255.0 2.8 fusion.89
  260.9 2.8 fusion.89
  266.7 2.8 fusion.89
  272.6 2.8 fusion.89
  278.5 2.8 fusion.89
  284.4 2.8 fusion.89
  297.8 53.9 %all-reduce = (f32[128]{0:T(128)S(1)}, f32[]{:T(128)}) all-reduce(f32[128]{0:T(128)S(1)} %multiply_reduce_fusion, f32[]{:T(128)S(6)} %add.117), channel_id=1, replica_groups=mesh['groups'=4,'asset_0'=32,'asset_1'=2] {'asset_0'}, use_global_device_ids=true, to_apply=%region_10.11 | all-reduce | flops 129 | bytes 1032 | tf_op jit(solution)/shard_map/psum | solution.py:66
  351.8 3.1 all-reduce.1
  (90 shorter events, 52.3 us)
Async XLA Ops:
  0.6 0.9 copy-start
  3.5 137.2 %all-to-all-start = ((bf16[32,64,256]{2,1,0:T(8,128)(2,1)}), bf16[32,64,256]{2,1,0:T(8,128)(2,1)S(1)}, u32[]{:S(2)}, u32[]{:S(2)}) async-start(bf16[32,64,256]{2,1,0:T(8,128)(2,1)} %broadcast_in_dim.37), calls=%async_computation | async-start | bytes 2097152 | tf_op jit(solution)/shard_map/all_to_all | solution.py:25
  146.4 1.5 copy-start.1
  146.4 1.5 copy-start.2
  146.4 1.5 copy-start.3
  146.4 1.5 copy-start.6
  147.9 23.4 %copy-start.5 = (f32[128]{0:T(128)S(1)}, f32[128]{0:T(128)}, u32[]{:S(2)}) copy-start(f32[128]{0:T(128)} %param.19) | copy-start | bytes 1540
  171.3 64.4 %copy-start.4 = (s32[4096]{0:T(1024)S(1)}, s32[4096]{0:T(1024)}, u32[]{:S(2)}) copy-start(s32[4096]{0:T(1024)} %param.18) | copy-start | bytes 49156
  204.7 28.4 %all-to-all-start.3 = ((f32[64,1,128]{2,1,0:T(1,128)}), f32[64,1,128]{2,1,0:T(1,128)S(1)}, u32[]{:S(2)}, u32[]{:S(2)}) async-start(f32[64,1,128]{2,1,0:T(1,128)} %broadcast_in_dim.39), calls=%async_computation.3 | async-start | bytes 65536 | tf_op jit(solution)/shard_map/all_to_all | solution.py:25
  248.1 1.0 copy-start.7
  253.9 1.0 copy-start.7
  259.8 1.0 copy-start.7
  265.7 1.0 copy-start.7
  271.6 1.0 copy-start.7
  277.4 1.0 copy-start.7
  283.3 1.0 copy-start.7
  289.2 1.0 copy-start.7
where the time goes:
time: 361 us; the launch traced here: 358 us
  waiting for transfers between devices  126 us (35%)
  blocking collectives  94 us (26%)
  matrix products  66.8 us (19%)
  starting transfers between devices  39.3 us (11%)
  other arithmetic  17 us (5%)
  local copies, waits for them, and re-layouts  8.23 us (2%)
  between operations  6.86 us (2%)
    all_to_all x2, waiting for transfers between devices, copy_for_each(): return lax.all_to_all(copies, axis, split_axis=0, concat_axis=0, tiled=True)  126 us
    psum x2, blocking collectives, over_axes(): x = lax.psum(x, axis)  57 us
    all_to_all x2, starting transfers between devices, copy_for_each(): return lax.all_to_all(copies, axis, split_axis=0, concat_axis=0, tiled=True)  39.3 us
    all_to_all x1, blocking collectives, summed_on_arrival(): tiles = lax.all_to_all(cut_along(x, dim, size), axis, 0, 0, tiled=True)  31.5 us
    dot_general x8, matrix products, pnl_one_block(): return jnp.dot(held, table, preferred_element_type=jnp.float32)  23.2 us
    dot_general x8, matrix products, exposure_of(): lax.dot_general(shock_rows, loadings, (((1,), (1,)), ((), ())), preferred...  22.1 us
    dot_general x8, matrix products, grad_one_block(): lax.dot_general(grad_exposure, shock_block, (((0,), (0,)), ((), ())), pre...  16.3 us
  transfers between devices with their start and end apart: 2, of which 2 were waited for; matrix products, arithmetic and copies ran while one was open for 0% of the time, Pallas kernels for 0%

commit v1 on v0

v1 whole, which is shorter than its diff:
```python
import math

import jax
import jax.numpy as jnp
import numpy as np
from jax import lax
from jax.experimental import pallas as pl
from jax.experimental.pallas import tpu as pltpu
from jax.sharding import Mesh
from jax.sharding import PartitionSpec as P

BAND = 32
CENTER = 166
FAR = 8
NEAR = 4
CLASSES = NEAR * 2
CHIPS = ("far", "near")
CLOSE = ("near", "core")
ASSET = ("far", "near", "core")
GROUPS_ASSET = ("groups", *ASSET)
LOG2 = math.log(2.0)
F32 = jnp.float32
BF16 = jnp.bfloat16
LANES = 128
TILE = 256
STEPS_Z = np.array([0, 0, 1, 3, 1, 3, 2, 2], np.int32)
OTHER = np.array([0, 1, 0, 0, 1, 1, 0, 1], np.int32)


def dot_of(a, b, dims, precision=None):
    return lax.dot_general(a, b, (dims, ((), ())), precision=precision, preferred_element_type=F32)


def forward_kernel(pieces, first, order_ref, *refs):
    shock_refs, refs = refs[:pieces], refs[pieces:]
    load_ref, conv_ref, hold_ref, desk_ref, price_ref = refs[:5]
    outs = refs[5:] if first else refs[10:]
    tanh_ref, bend_ref, pnl_ref, turned_ref, sums_ref, rows, table = outs
    step = pl.program_id(0)
    piece = shock_refs[0].shape[0]
    assets = load_ref.shape[0]
    desks = price_ref.shape[1]

    @pl.when(step == 0)
    def _():
        for i in range(pieces):
            rows[i * piece : (i + 1) * piece, :] = shock_refs[i][...]
        desk = lax.broadcasted_iota(jnp.int32, (desks, assets), 0)
        table[...] = jnp.where(desk == desk_ref[...], 1.0, 0.0).astype(BF16)

    size = tanh_ref.shape[0]
    shocks = rows[pl.ds(pl.multiple_of(step * size, size), size), :]
    turned_ref[...] = shocks.T
    pnl = jnp.zeros((size, desks), F32)
    for low in range(0, assets, TILE):
        part = slice(low, low + TILE)
        exposure = dot_of(shocks, load_ref[part, :], ((1,), (1,)))
        size_of = jnp.abs(exposure)
        bend = size_of + (jnp.log(1.0 + jnp.exp(-2.0 * size_of)) - LOG2)
        held = hold_ref[:, part] * (exposure + conv_ref[:, part] * bend)
        tanh_ref[:, part] = jnp.tanh(exposure).astype(BF16)
        bend_ref[:, part] = bend.astype(BF16)
        pnl = pnl + dot_of(held.astype(BF16), table[:, part], ((1,), (1,)))
    pnl_ref[...] = pnl
    row = lax.broadcasted_iota(jnp.int32, (8, desks), 0)
    weigh = jnp.where(row == 0, -1.0, jnp.where(row == 1, price_ref[...], 0.0))
    sums = dot_of(weigh, pnl, ((1,), (1,)), lax.Precision.HIGHEST)
    lines = size // LANES
    half = step % 2
    for part in range(2):
        for line in range(lines):
            sums_ref[0, pl.ds(part * 4 + half * lines + line, 1), :] = sums[
                part : part + 1, line * LANES : (line + 1) * LANES
            ]


def forward_call(shocks, place, order, loadings, convexity, holdings, desk_map, prices, held):
    pieces, piece, factors = len(shocks), *shocks[0].shape
    scenarios = piece * CLASSES
    assets, desks = loadings.shape[0], prices.shape[1]
    size = piece // 2
    first = held is None
    base = place * 2
    whole = lambda shape: pl.BlockSpec(shape, lambda i, o: (0, 0))
    out_shape = (
        jax.ShapeDtypeStruct((scenarios, assets), BF16),
        jax.ShapeDtypeStruct((scenarios, assets), BF16),
        jax.ShapeDtypeStruct((scenarios, desks), F32),
        jax.ShapeDtypeStruct((factors, scenarios), BF16),
        jax.ShapeDtypeStruct((CLASSES, 8, LANES), F32),
    )
    out_specs = (
        pl.BlockSpec((size, assets), lambda i, o: (base + i, 0)),
        pl.BlockSpec((size, assets), lambda i, o: (base + i, 0)),
        pl.BlockSpec((size, desks), lambda i, o: (base + i, 0)),
        pl.BlockSpec((factors, size), lambda i, o: (0, base + i)),
        pl.BlockSpec((1, 8, LANES), lambda i, o: (o[place + i // 2], 0, 0)),
    )
    in_specs = [whole((piece, factors))] * pieces + [
        whole((assets, factors)),
        whole((1, assets)),
        whole((1, assets)),
        whole((1, assets)),
        whole((1, desks)),
    ]
    operands = [*shocks, loadings, convexity, holdings, desk_map, prices]
    aliases = {}
    if not first:
        aliases = {1 + len(operands) + i: i for i in range(5)}
        in_specs += [pl.BlockSpec(memory_space=pl.ANY)] * 5
        operands += list(held)
    return pl.pallas_call(
        lambda *refs: forward_kernel(pieces, first, *refs),
        grid_spec=pltpu.PrefetchScalarGridSpec(
            num_scalar_prefetch=1,
            grid=(pieces * 2,),
            in_specs=in_specs,
            out_specs=out_specs,
            scratch_shapes=[
                pltpu.VMEM((pieces * piece, factors), BF16),
                pltpu.VMEM((desks, assets), BF16),
            ],
        ),
        out_shape=out_shape,
        input_output_aliases=aliases,
        compiler_params=pltpu.CompilerParams(dimension_semantics=("arbitrary",)),
        cost_estimate=pl.CostEstimate(
            flops=2 * pieces * piece * assets * (factors + desks),
            bytes_accessed=pieces * piece * assets * 4,
            transcendentals=3 * pieces * piece * assets,
        ),
        name=f"forward_{place}",
    )(order, *operands)


def total(x):
    x = jnp.sum(x, axis=0, keepdims=True)
    x = jnp.sum(x, axis=1, keepdims=True)
    return jnp.sum(x, axis=2, keepdims=True)


def tail_of(losses, valued, ranks):
    scenarios = losses.size
    place = (
        lax.broadcasted_iota(jnp.int32, losses.shape, 0) * (losses.shape[1] * LANES)
        + lax.broadcasted_iota(jnp.int32, losses.shape, 1) * LANES
        + lax.broadcasted_iota(jnp.int32, losses.shape, 2)
    )
    offsets = (ranks.astype(F32) - CENTER) / BAND
    every = (place.astype(F32) - CENTER) / BAND
    kernel = jnp.exp(-0.5 * offsets * offsets) / total(jnp.exp(-0.5 * every * every))
    quantile = total(kernel * losses)
    average = total(losses) / scenarios
    centred = losses - average
    smoothing = 0.3 * jnp.sqrt(total(centred * centred) / scenarios + 1e-06)
    scores = (losses - quantile) / smoothing
    weights = 1.0 / (1.0 + jnp.exp(-scores))
    weight_total = total(weights)
    objective = -total(weights * valued) / weight_total
    slopes = (-valued - objective) / weight_total * weights * (1.0 - weights)
    grad_quant = -total(slopes) / smoothing
    grad_band = -total(slopes * scores) / smoothing
    grad_loss = (
        slopes / smoothing
        + kernel * grad_quant
        + grad_band * 0.09 * centred / (scenarios * smoothing)
    )
    return (-scenarios * weights / weight_total, -scenarios * grad_loss)


def backward_kernel(order_ref, *refs):
    sums_ref, ranks_ref, tanh_ref, bend_ref, pnl_ref, turned_ref = refs[:6]
    conv_ref, hold_ref, desk_ref, price_ref = refs[6:10]
    raw_ref, line_ref, last_ref, scaled, lines, wide, line_sums, both = refs[10:]
    step = pl.program_id(0)
    factors, scenarios = turned_ref.shape
    desks = price_ref.shape[0]
    piece = scenarios // CLASSES
    cuts = piece // LANES

    @pl.when(step == 0)
    def _():
        w, g = tail_of(sums_ref[:, 0:cuts, :], sums_ref[:, cuts : 2 * cuts, :], ranks_ref[...])
        both[:, 0:cuts, :] = w
        both[:, cuts : 2 * cuts, :] = g
        alloc = jnp.zeros((8, desks), F32)
        sum_w = jnp.zeros((factors, LANES), F32)
        sum_g = jnp.zeros((factors, LANES), F32)
        for i in range(CLASSES):
            kind = order_ref[i]
            rows_w, rows_g = [], []
            for j in range(cuts):
                span = slice(i * piece + j * LANES, i * piece + (j + 1) * LANES)
                turned = turned_ref[:, span].astype(F32)
                row_w = both[kind, j : j + 1, :]
                row_g = both[kind, cuts + j : cuts + j + 1, :]
                by_w = turned * row_w
                by_g = turned * row_g
                sum_w = sum_w + by_w
                sum_g = sum_g + by_g
                scaled[0:factors, span] = by_w.astype(BF16)
                scaled[factors : 2 * factors, span] = by_g.astype(BF16)
                rows_w.append(row_w)
                rows_g.append(row_g)
            row_w = jnp.concatenate(rows_w, axis=1)
            row_g = jnp.concatenate(rows_g, axis=1)
            wide_w = jnp.broadcast_to(row_w, (8, piece))
            wide_g = jnp.broadcast_to(row_g, (8, piece))
            place = lax.broadcasted_iota(jnp.int32, (8, piece), 0)
            value = jnp.where(place < 2, wide_w, wide_g)
            high = value.astype(BF16).astype(F32)
            lines[:, i * piece : (i + 1) * piece] = jnp.where(place % 2 == 0, high, value - high).astype(
                BF16
            )
            alloc = alloc + dot_of(
                wide_w, pnl_ref[i * piece : (i + 1) * piece, :], ((1,), (0,)), lax.Precision.HIGHEST
            )
        wide[:, 0:1] = jnp.sum(sum_w, axis=1, keepdims=True)
        wide[:, 1:2] = jnp.sum(sum_g, axis=1, keepdims=True)
        last_ref[:, 0:desks] = alloc[0:1, :] / scenarios
        last_ref[:, desks : 2 * desks] = jnp.zeros((1, desks), F32)

    held = hold_ref[...]
    desk = lax.broadcasted_iota(jnp.int32, (desks, held.shape[1]), 0)
    prices = jnp.sum(jnp.where(desk == desk_ref[...], price_ref[...], 0.0), axis=0, keepdims=True)
    curved = dot_of(scaled[...], tanh_ref[...], ((1,), (0,)))
    bent = dot_of(lines[...], bend_ref[...], ((1,), (0,)))
    line = held * (prices * (bent[0:1, :] + bent[1:2, :]) + (bent[2:3, :] + bent[3:4, :]))
    raw = (conv_ref[...] * held) * (prices * curved[0:factors, :] + curved[factors:, :]) + held * (
        prices * wide[:, 0:1] + wide[:, 1:2]
    )
    raw_ref[...] = raw.T
    line_ref[...] = line
    squares = jnp.sum(raw * raw, axis=0, keepdims=True) + line * line
    for low in range(0, squares.shape[1], desks):
        last_ref[:, desks : 2 * desks] += squares[:, low : low + desks]


def backward_call(order, sums, ranks, held, convexity, holdings, desk_map, prices):
    tanh, bend, pnl, turned = held
    scenarios, assets = tanh.shape
    factors, desks = turned.shape[0], pnl.shape[1]
    whole = lambda *shape: pl.BlockSpec(shape, lambda i, o: (0,) * len(shape))
    line = pl.BlockSpec((1, TILE), lambda i, o: (0, i))
    column = pl.BlockSpec((scenarios, TILE), lambda i, o: (0, i))
    return pl.pallas_call(
        backward_kernel,
        grid_spec=pltpu.PrefetchScalarGridSpec(
            num_scalar_prefetch=1,
            grid=(assets // TILE,),
            in_specs=[
                whole(*sums.shape),
                whole(*ranks.shape),
                column,
                column,
                whole(scenarios, desks),
                whole(factors, scenarios),
                line,
                line,
                line,
                whole(desks, 1),
            ],
            out_specs=(
                pl.BlockSpec((TILE, factors), lambda i, o: (i, 0)),
                line,
                whole(1, 2 * desks),
            ),
            scratch_shapes=[
                pltpu.VMEM((2 * factors, scenarios), BF16),
                pltpu.VMEM((8, scenarios), BF16),
                pltpu.VMEM((factors, 2), F32),
                pltpu.VMEM((8, LANES), F32),
                pltpu.VMEM(sums.shape, F32),
            ],
        ),
        out_shape=(
            jax.ShapeDtypeStruct((assets, factors), F32),
            jax.ShapeDtypeStruct((1, assets), F32),
            jax.ShapeDtypeStruct((1, 2 * desks), F32),
        ),
        compiler_params=pltpu.CompilerParams(dimension_semantics=("arbitrary",)),
        cost_estimate=pl.CostEstimate(
            flops=4 * scenarios * assets * factors,
            bytes_accessed=scenarios * assets * 4,
            transcendentals=0,
        ),
        name="backward",
    )(order, sums, ranks, tanh, bend, pnl, turned, convexity, holdings, desk_map, prices)


def scale_kernel(entries, parts_ref, raw_ref, line_ref, alloc_ref, grad_ref, conv_ref):
    whole = jnp.sum(parts_ref[...], axis=0)
    desks = alloc_ref.shape[1]
    alloc_ref[...] = whole[:, 0:desks]
    squares = jnp.sum(whole[:, desks:], axis=1, keepdims=True)
    factor = lax.rsqrt(squares / entries + 1e-06)
    grad_ref[...] = raw_ref[...] * factor
    conv_ref[...] = line_ref[...] * factor


def scale_call(parts, raw, line, entries):
    desks = parts.shape[2] // 2
    return pl.pallas_call(
        lambda *refs: scale_kernel(entries, *refs),
        out_shape=(
            jax.ShapeDtypeStruct((1, desks), F32),
            jax.ShapeDtypeStruct(raw.shape, F32),
            jax.ShapeDtypeStruct(line.shape, F32),
        ),
        name="scale",
    )(parts, raw, line)


def for_each(x, axis):
    return lax.all_to_all(
        jnp.broadcast_to(x, (lax.axis_size(axis), *x.shape)), axis, 0, 0, tiled=True
    )


def shards(scen_draws, factor_mix, loadings, convexity, holdings, desk_map, ranks, desk_prices):
    chips = FAR * NEAR
    near, core = lax.axis_index("near"), lax.axis_index("core")
    order = ((near + STEPS_Z) % NEAR) * 2 + (core + OTHER) % 2
    up = [(i, (i - 1) % chips) for i in range(chips)]
    down = [(i, (i + 1) % chips) for i in range(chips)]
    swap = lambda x: lax.ppermute(x, "core", [(0, 1), (1, 0)])
    from_up = lambda x: lax.ppermute(x, CHIPS, up)
    from_down = lambda x: lax.ppermute(x, CHIPS, down)

    local = jnp.dot(scen_draws, factor_mix, preferred_element_type=F32).astype(BF16)
    own = for_each(local, "far").reshape(-1, local.shape[1])
    half = own.shape[0] // 2
    lines = [x.reshape(1, -1) for x in (convexity, holdings, desk_map)]
    forward = lambda shocks, place, held: forward_call(
        shocks, place, order, loadings, *lines, desk_prices.reshape(1, -1), held
    )
    next_up, next_down = from_up(own), from_down(own)
    own_other = swap(own)
    held = forward([own, own_other], 0, None)
    next_up, next_down, held = lax.optimization_barrier((next_up, next_down, held))
    two_up = from_up(next_up[:half])
    two_down = from_down(next_down[half:])
    up_other, down_other = swap(next_up), swap(next_down)
    held = forward([next_up, next_down, up_other, down_other], 2, held)
    two_up, two_down, held = lax.optimization_barrier((two_up, two_down, held))
    two = jnp.concatenate([two_up, two_down])
    held = forward([two, swap(two)], 6, held)

    mine = jnp.sum(lax.all_to_all(held[4], CLOSE, 0, 0, tiled=True), axis=0)
    mine = jnp.sum(for_each(mine, "far"), axis=0)
    sums = for_each(mine, CLOSE)
    placed = ranks.reshape(FAR, CLASSES, -1).transpose(1, 0, 2).reshape(CLASSES, -1, LANES)
    raw, line, last = backward_call(
        order, sums, placed, held[:4], *lines, desk_prices.reshape(-1, 1)
    )
    entries = loadings.shape[0] * lax.axis_size(ASSET) * (loadings.shape[1] + 1)
    alloc, grad, conv = scale_call(for_each(last, ASSET), raw, line, entries)
    return (alloc.reshape(-1), grad, conv.reshape(-1))


def solution(mesh):
    torus = Mesh(
        mesh.devices.reshape(mesh.shape["groups"], FAR, NEAR, 2), ("groups", *ASSET)
    )
    return jax.shard_map(
        shards,
        mesh=torus,
        in_specs=(
            P(GROUPS_ASSET, None),
            P(),
            P(GROUPS_ASSET, None),
            P(GROUPS_ASSET),
            P(GROUPS_ASSET),
            P(GROUPS_ASSET),
            P("groups"),
            P("groups"),
        ),
        out_specs=(P("groups"), P(GROUPS_ASSET, None), P(GROUPS_ASSET)),
        check_vma=False,
    )
```

time: 361 us -> 211 us (0.58)
  waiting for transfers between devices: 126 us -> 5.36 us
  matrix products: 66.8 us -> 0.89 us
  Pallas kernels: 0 us -> 44.7 us
  blocking collectives: 94 us -> 134 us
  starting transfers between devices: 39.3 us -> 16.2 us
  other arithmetic: 17 us -> 1.21 us
  between operations: 6.86 us -> 0.81 us
    all_to_all x2 -> x1, waiting for transfers between devices: 126 us -> 3.83 us  [for_each(): lax.all_to_all(jnp.broadcast_to(x, (lax.axis_size(axis), *x.shape)), axis...]
    all_to_all x2 -> x4, blocking collectives: 36.9 us -> 134 us  [the longest x3 124 us: for_each(): lax.all_to_all(jnp.broadcast_to(x, (lax.axis_size(axis), *x.shape)), axis...]
    dot_general x33 -> x1, matrix products: 66.8 us -> 0.89 us  [shards(): jnp.dot(scen_draws, factor_mix, preferred_element_type=F32).astype(BF16)]
    psum x2 -> x0, blocking collectives: 57 us -> none  [over_axes(): x = lax.psum(x, axis)]
    pallas_call x0 -> x5, Pallas kernels: none -> 44.7 us  [the longest x3 26.8 us: forward_call(): pl.pallas_call(lambda *refs: forward_kernel(pieces, first, *refs), grid_s...]
    all_to_all x2 -> x1, starting transfers between devices: 39.3 us -> 3.72 us  [for_each(): lax.all_to_all(jnp.broadcast_to(x, (lax.axis_size(axis), *x.shape)), axis...]
    ppermute x0 -> x8, starting transfers between devices: none -> 12.4 us  [the longest x2 6.36 us: shards(): from_up = lambda x: lax.ppermute(x, CHIPS, up)]
    reduce_sum x11 -> x2, other arithmetic: 9.67 us -> 0.02 us  [the longest x1 0.01 us: shards(): mine = jnp.sum(lax.all_to_all(held[4], CLOSE, 0, 0, tiled=True), axis=0)]
  transfers between devices with their start and end apart: 2 -> 9, of which waited for: 2 -> 2; matrix products, arithmetic and copies ran while one was open for 0% -> 1% of each run, Pallas kernels for 0% -> 9%
where the time goes in v1:
time: 211 us
  blocking collectives  134 us (64%)
  Pallas kernels  44.7 us (21%)
  starting transfers between devices  16.2 us (8%)
  local copies, waits for them, and re-layouts  7.27 us (3%)
  waiting for transfers between devices  5.36 us (3%)
    all_to_all x3, blocking collectives, for_each(): lax.all_to_all(jnp.broadcast_to(x, (lax.axis_size(axis), *x.shape)), axis...  124 us
    pallas_call x3, Pallas kernels, forward_call(): pl.pallas_call(lambda *refs: forward_kernel(pieces, first, *refs), grid_s...  26.8 us
    pallas_call x1, Pallas kernels, backward_call(): pl.pallas_call(backward_kernel, grid_spec=pltpu.PrefetchScalarGridSpec(nu...  15.5 us
    all_to_all x1, blocking collectives, shards(): mine = jnp.sum(lax.all_to_all(held[4], CLOSE, 0, 0, tiled=True), axis=0)  10.9 us
    ppermute x2, starting transfers between devices, shards(): from_up = lambda x: lax.ppermute(x, CHIPS, up)  6.36 us
    ppermute x2, starting transfers between devices, shards(): from_down = lambda x: lax.ppermute(x, CHIPS, down)  5.3 us
    unnamed x25, local copies, waits for them, and re-layouts  4.36 us
  transfers between devices with their start and end apart: 9, of which 2 were waited for; matrix products, arithmetic and copies ran while one was open for 1% of the time, Pallas kernels for 9%

profile of v1, /device:TPU:38, one launch (start us, length us, event | category | flops | bytes accessed | tf_op | source)
XLA Modules:
  0.0 210.8 jit_solution(7412311522473153395)
XLA Ops:
  0.6 0.9 copy-done
  1.5 0.9 convolution_convert_fusion
  2.5 63.6 %all_to_all.25 = bf16[8,64,256]{2,1,0:T(8,128)(2,1)S(1)} all-to-all(bf16[8,64,256]{2,1,0:T(8,128)(2,1)S(1)} %broadcast_in_dim.12), channel_id=1, replica_groups=mesh['groups'=4,'far'=8,'near'=4,'core'=2] {'far'}, dimensions={0} | all-to-all | bytes 524288 | tf_op jit(solution)/shard_map/all_to_all | solution.py:315
  66.1 4.5 %collective-permute-start = (bf16[512,256]{1,0:T(8,128)(2,1)S(1)}, bf16[512,256]{1,0:T(8,128)(2,1)S(1)}, u32[]{:S(2)}, u32[]{:S(2)}) collective-permute-start(bf16[512,256]{1,0:T(8,128)(2,1)S(1)} %bitcast.13), channel_id=1, source_target_pairs={{0,62},{2,0},{4,2},{6,4},{8,6},{10,8},{12,10},{14,12},{16,14},{18,... | collective-permute-start | bytes 786440 | tf_op jit(solution)/shard_map/ppermute | solution.py:327
  70.5 5.0 %collective-permute-start.1 = (bf16[512,256]{1,0:T(8,128)(2,1)S(1)}, bf16[512,256]{1,0:T(8,128)(2,1)S(1)}, u32[]{:S(2)}, u32[]{:S(2)}) collective-permute-start(bf16[512,256]{1,0:T(8,128)(2,1)S(1)} %bitcast.14), channel_id=1, source_target_pairs={{0,2},{2,4},{4,6},{6,8},{8,10},{10,12},{12,14},{14,16},{16,18},{18... | collective-permute-start | bytes 786440 | tf_op jit(solution)/shard_map/ppermute | solution.py:328
  75.6 1.2 fusion.refs_0_.order_ref
  76.8 0.7 copy-done.11
  77.5 7.3 %forward_0.1 = (bf16[4096,1024]{1,0:T(8,128)(2,1)}, bf16[4096,1024]{1,0:T(8,128)(2,1)}, f32[4096,128]{1,0:T(8,128)}, bf16[256,4096]{1,0:T(8,128)(2,1)}, f32[8,8,128]{2,1,0:T(8,128)}) custom-call(s32[8]{0:T(128)} %fusion.refs_0_.order_ref, bf16[512,256]{1,0:T(8,128)(2,1)} %bitcast.15, bf16[512,256]{1,0:T(8,128)(2,1)} %copy-done.11, ...), custom_call_target="tpu_custom_call" | custom-call | flops 805306368 | bytes 4194304 | tf_op jit(solution)/shard_map/forward_0/pallas_call | solution.py:112
  85.5 1.9 collective-permute-start.3
  88.4 0.7 copy-done.5
  89.1 12.1 %forward_2.1 = (bf16[4096,1024]{1,0:T(8,128)(2,1)}, bf16[4096,1024]{1,0:T(8,128)(2,1)}, f32[4096,128]{1,0:T(8,128)}, bf16[256,4096]{1,0:T(8,128)(2,1)}, f32[8,8,128]{2,1,0:T(8,128)}) custom-call(s32[8]{0:T(128)} %fusion.refs_0_.order_ref, bf16[512,256]{1,0:T(8,128)(2,1)} %copy-done.1, ...), custom_call_target="tpu_custom_call", output_to_operand_aliasing={{0}: (10, {}), {1}: (11, {}), {2}: (12, {}), {3}: (13, {}),... | custom-call | flops 1610612736 | bytes 8388608 | tf_op jit(solution)/shard_map/forward_2/pallas_call | solution.py:112
  101.4 1.5 collective-permute-done.7.refs_2_
  102.9 0.7 copy-done.6
  103.6 7.4 %forward_6.1 = (bf16[4096,1024]{1,0:T(8,128)(2,1)}, bf16[4096,1024]{1,0:T(8,128)(2,1)}, f32[4096,128]{1,0:T(8,128)}, bf16[256,4096]{1,0:T(8,128)(2,1)}, f32[8,8,128]{2,1,0:T(8,128)}) custom-call(s32[8]{0:T(128)} %fusion.refs_0_.order_ref, bf16[512,256]{1,0:T(8,128)(2,1)} %copy-done.3, ...), custom_call_target="tpu_custom_call", output_to_operand_aliasing={{0}: (8, {}), {1}: (9, {}), {2}: (10, {}), {3}: (11, {}), {... | custom-call | flops 805306368 | bytes 4194304 | tf_op jit(solution)/shard_map/forward_6/pallas_call | solution.py:112
  111.0 10.9 %all_to_all.26 = f32[8,8,128]{2,1,0:T(8,128)S(1)} all-to-all(f32[8,8,128]{2,1,0:T(8,128)} %get-tuple-element.62), channel_id=1, replica_groups=mesh['groups'=4,'far'=8,'near'=4,'core'=2] {'near','core'}, dimensions={0} | all-to-all | bytes 65536 | tf_op jit(solution)/shard_map/all_to_all | solution.py:349
  121.9 28.9 %all_to_all.27 = f32[8,8,128]{2,1,0:T(8,128)S(1)} all-to-all(f32[8,8,128]{2,1,0:T(8,128)S(1)} %broadcast_in_dim.13), channel_id=1, replica_groups=mesh['groups'=4,'far'=8,'near'=4,'core'=2] {'far'}, dimensions={0} | all-to-all | bytes 65536 | tf_op jit(solution)/shard_map/all_to_all | solution.py:315
  151.4 3.7 %all-to-all-start.3 = ((f32[8,8,128]{2,1,0:T(8,128)}), f32[8,8,128]{2,1,0:T(8,128)S(1)}, u32[]{:S(2)}, u32[]{:S(2)}) async-start(f32[8,8,128]{2,1,0:T(8,128)} %broadcast_in_dim.14), calls=%async_computation.3 | async-start | bytes 65536 | tf_op jit(solution)/shard_map/all_to_all | solution.py:315
  155.2 0.7 reshape.45.refs_1_
  155.9 0.7 copy.27.refs_9_
  156.6 3.8 %all-to-all-done.3.refs_0_ = f32[8,8,128]{2,1,0:T(8,128)S(1)} async-done(((f32[8,8,128]{2,1,0:T(8,128)}), f32[8,8,128]{2,1,0:T(8,128)S(1)}, u32[]{:S(2)}, u32[]{:S(2)}) %all-to-all-start.3) | async-done | bytes 32800 | tf_op jit(solution)/shard_map/all_to_all | solution.py:315
  161.1 15.5 %backward.1 = (f32[1024,256]{1,0:T(8,128)}, f32[1,1024]{1,0:T(1,128)}, f32[1,256]{1,0:T(1,128)}) custom-call(s32[8]{0:T(128)} %fusion.refs_0_.order_ref, f32[8,8,128]{2,1,0:T(8,128)} %copy-done.8, s32[8,4,128]{2,1,0:T(4,128)} %reshape.45.refs_1_, bf16[4096,1024]{1,0:T(8,128)(2,1)} %get-tuple-element.63.refs_2_, ...), custom_call_target="tpu_custom_call" | custom-call | flops 4294967296 | bytes 16777216 | tf_op jit(solution)/shard_map/backward/pallas_call | solution.py:246
  176.5 0.7 broadcast_in_dim.15
  177.3 31.1 %all_to_all.28.refs_0_ = f32[64,1,256]{2,1,0:T(1,128)} all-to-all(f32[64,1,256]{2,1,0:T(1,128)S(1)} %broadcast_in_dim.15), channel_id=1, replica_groups=mesh['groups'=4,'far'=8,'near'=4,'core'=2] {'far','near','core'}, dimensions={0} | all-to-all | bytes 131072 | tf_op jit(solution)/shard_map/all_to_all | solution.py:315
  208.4 2.4 %scale.1 = (f32[1,128]{1,0:T(1,128)}, f32[1024,256]{1,0:T(8,128)}, f32[1,1024]{1,0:T(1,128)}) custom-call(f32[64,1,256]{2,1,0:T(1,128)} %all_to_all.28.refs_0_, f32[1024,256]{1,0:T(8,128)} %get-tuple-element.68.refs_1_, f32[1,1024]{1,0:T(1,128)} %get-tuple-element.69.refs_2_), custom_call_target="tpu_custom_call" | custom-call | tf_op jit(solution)/shard_map/scale/pallas_call | solution.py:303
  (43 shorter events, 3.2 us)
Async XLA Ops:
  0.6 0.9 copy-start
  66.1 10.7 %copy-start.7 = (bf16[8,64,256]{2,1,0:T(8,128)(2,1)}, bf16[8,64,256]{2,1,0:T(8,128)(2,1)S(1)}, u32[]{:S(2)}) copy-start(bf16[8,64,256]{2,1,0:T(8,128)(2,1)S(1)} %all_to_all.25) | copy-start | bytes 786436
  66.1 10.7 %collective-permute-start.2 = (bf16[512,256]{1,0:T(8,128)(2,1)S(1)}, bf16[512,256]{1,0:T(8,128)(2,1)S(1)}, u32[]{:S(2)}, u32[]{:S(2)}) collective-permute-start(bf16[512,256]{1,0:T(8,128)(2,1)S(1)} %bitcast.12), channel_id=1, source_target_pairs={{0,1},{1,0},{2,3},{3,2},{4,5},{5,4},{6,7},{7,6},{8,9},{9,8},{10,11... | collective-permute-start | bytes 786440 | tf_op jit(solution)/shard_map/ppermute | solution.py:326
  66.1 18.7 %collective-permute-start = (bf16[512,256]{1,0:T(8,128)(2,1)S(1)}, bf16[512,256]{1,0:T(8,128)(2,1)S(1)}, u32[]{:S(2)}, u32[]{:S(2)}) collective-permute-start(bf16[512,256]{1,0:T(8,128)(2,1)S(1)} %bitcast.13), channel_id=1, source_target_pairs={{0,62},{2,0},{4,2},{6,4},{8,6},{10,8},{12,10},{14,12},{16,14},{18,... | collective-permute-start | bytes 786440 | tf_op jit(solution)/shard_map/ppermute | solution.py:327
  70.5 14.3 %collective-permute-start.1 = (bf16[512,256]{1,0:T(8,128)(2,1)S(1)}, bf16[512,256]{1,0:T(8,128)(2,1)S(1)}, u32[]{:S(2)}, u32[]{:S(2)}) collective-permute-start(bf16[512,256]{1,0:T(8,128)(2,1)S(1)} %bitcast.14), channel_id=1, source_target_pairs={{0,2},{2,4},{4,6},{6,8},{8,10},{10,12},{12,14},{14,16},{16,18},{18... | collective-permute-start | bytes 786440 | tf_op jit(solution)/shard_map/ppermute | solution.py:328
  76.8 0.7 copy-start.11
  84.8 2.9 %copy-start.1 = (bf16[512,256]{1,0:T(8,128)(2,1)}, bf16[512,256]{1,0:T(8,128)(2,1)S(1)}, u32[]{:S(2)}) copy-start(bf16[512,256]{1,0:T(8,128)(2,1)S(1)} %collective-permute-done.refs_1_) | copy-start | bytes 786436
  84.8 2.9 %copy-start.2 = (bf16[512,256]{1,0:T(8,128)(2,1)}, bf16[512,256]{1,0:T(8,128)(2,1)S(1)}, u32[]{:S(2)}) copy-start(bf16[512,256]{1,0:T(8,128)(2,1)S(1)} %collective-permute-done.1.refs_2_) | copy-start | bytes 786436
  84.8 2.8 %collective-permute-start.5 = (bf16[512,256]{1,0:T(8,128)(2,1)S(1)}, bf16[512,256]{1,0:T(8,128)(2,1)S(1)}, u32[]{:S(2)}, u32[]{:S(2)}) collective-permute-start(bf16[512,256]{1,0:T(8,128)(2,1)S(1)} %collective-permute-done.refs_1_), channel_id=1, source_target_pairs={{0,1},{1,0},{2,3},{3,2},{4,5},{5,4},{6,7},{7,6},{8,9},{9,8},{10,11... | collective-permute-start | bytes 786440 | tf_op jit(solution)/shard_map/ppermute | solution.py:326
  85.1 2.6 %collective-permute-start.6 = (bf16[512,256]{1,0:T(8,128)(2,1)S(1)}, bf16[512,256]{1,0:T(8,128)(2,1)S(1)}, u32[]{:S(2)}, u32[]{:S(2)}) collective-permute-start(bf16[512,256]{1,0:T(8,128)(2,1)S(1)} %collective-permute-done.1.refs_2_), channel_id=1, source_target_pairs={{0,1},{1,0},{2,3},{3,2},{4,5},{5,4},{6,7},{7,6},{8,9},{9,8},{10,11... | collective-permute-start | bytes 786440 | tf_op jit(solution)/shard_map/ppermute | solution.py:326
  85.5 15.7 %collective-permute-start.3 = (bf16[256,256]{1,0:T(8,128)(2,1)S(1)}, bf16[256,256]{1,0:T(8,128)(2,1)S(1)}, u32[]{:S(2)}, u32[]{:S(2)}) collective-permute-start(bf16[256,256]{1,0:T(8,128)(2,1)S(1)} %slice.6), channel_id=1, source_target_pairs={{0,62},{2,0},{4,2},{6,4},{8,6},{10,8},{12,10},{14,12},{16,14},{18,... | collective-permute-start | bytes 393224 | tf_op jit(solution)/shard_map/ppermute | solution.py:327
  87.4 13.8 %collective-permute-start.4 = (bf16[256,256]{1,0:T(8,128)(2,1)S(1)}, bf16[256,256]{1,0:T(8,128)(2,1)S(1)}, u32[]{:S(2)}, u32[]{:S(2)}) collective-permute-start(bf16[256,256]{1,0:T(8,128)(2,1)S(1)} %slice.7), channel_id=1, source_target_pairs={{0,2},{2,4},{4,6},{6,8},{8,10},{10,12},{12,14},{14,16},{16,18},{18... | collective-permute-start | bytes 393224 | tf_op jit(solution)/shard_map/ppermute | solution.py:328
  87.7 0.7 copy-start.4
  88.4 0.7 copy-start.5
  101.2 1.7 copy-start.3
  101.2 53.9 %copy-start.9 = (s32[4096]{0:T(1024)S(1)}, s32[4096]{0:T(1024)}, u32[]{:S(2)}) copy-start(s32[4096]{0:T(1024)} %param.16) | copy-start | bytes 49156
  101.3 54.6 %copy-start.10 = (f32[128]{0:T(128)S(1)}, f32[128]{0:T(128)}, u32[]{:S(2)}) copy-start(f32[128]{0:T(128)} %param.17) | copy-start | bytes 1540
  101.3 1.7 collective-permute-start.7
  102.9 0.7 copy-start.6
  151.4 9.1 %all-to-all-start.3 = ((f32[8,8,128]{2,1,0:T(8,128)}), f32[8,8,128]{2,1,0:T(8,128)S(1)}, u32[]{:S(2)}, u32[]{:S(2)}) async-start(f32[8,8,128]{2,1,0:T(8,128)} %broadcast_in_dim.14), calls=%async_computation.3 | async-start | bytes 65536 | tf_op jit(solution)/shard_map/all_to_all | solution.py:315
  160.5 0.6 copy-start.8

commit v2 on v1

--- a/solution.py
+++ b/solution.py
@@ -23,6 +23,9 @@
 BF16 = jnp.bfloat16
 LANES = 128
 TILE = 256
+FORWARD_VMEM = 16 << 20
+BACKWARD_VMEM = 20 << 20
+SCALE_VMEM = 8 << 20
 STEPS_Z = np.array([0, 0, 1, 3, 1, 3, 2, 2], np.int32)
 OTHER = np.array([0, 1, 0, 0, 1, 1, 0, 1], np.int32)
 
@@ -66,10 +69,9 @@
     weigh = jnp.where(row == 0, -1.0, jnp.where(row == 1, price_ref[...], 0.0))
     sums = dot_of(weigh, pnl, ((1,), (1,)), lax.Precision.HIGHEST)
     lines = size // LANES
-    half = step % 2
     for part in range(2):
         for line in range(lines):
-            sums_ref[0, pl.ds(part * 4 + half * lines + line, 1), :] = sums[
+            sums_ref[0, part * lines + line : part * lines + line + 1, :] = sums[
                 part : part + 1, line * LANES : (line + 1) * LANES
             ]
 
@@ -78,9 +80,9 @@
     pieces, piece, factors = len(shocks), *shocks[0].shape
     scenarios = piece * CLASSES
     assets, desks = loadings.shape[0], prices.shape[1]
-    size = piece // 2
+    size = piece
     first = held is None
-    base = place * 2
+    base = place
     whole = lambda shape: pl.BlockSpec(shape, lambda i, o: (0, 0))
     out_shape = (
         jax.ShapeDtypeStruct((scenarios, assets), BF16),
@@ -94,7 +96,7 @@
         pl.BlockSpec((size, assets), lambda i, o: (base + i, 0)),
         pl.BlockSpec((size, desks), lambda i, o: (base + i, 0)),
         pl.BlockSpec((factors, size), lambda i, o: (0, base + i)),
-        pl.BlockSpec((1, 8, LANES), lambda i, o: (o[place + i // 2], 0, 0)),
+        pl.BlockSpec((1, 8, LANES), lambda i, o: (o[place + i], 0, 0)),
     )
     in_specs = [whole((piece, factors))] * pieces + [
         whole((assets, factors)),
@@ -113,7 +115,7 @@
         lambda *refs: forward_kernel(pieces, first, *refs),
         grid_spec=pltpu.PrefetchScalarGridSpec(
             num_scalar_prefetch=1,
-            grid=(pieces * 2,),
+            grid=(pieces,),
             in_specs=in_specs,
             out_specs=out_specs,
             scratch_shapes=[
@@ -123,7 +125,9 @@
         ),
         out_shape=out_shape,
         input_output_aliases=aliases,
-        compiler_params=pltpu.CompilerParams(dimension_semantics=("arbitrary",)),
+        compiler_params=pltpu.CompilerParams(
+            dimension_semantics=("arbitrary",), vmem_limit_bytes=FORWARD_VMEM
+        ),
         cost_estimate=pl.CostEstimate(
             flops=2 * pieces * piece * assets * (factors + desks),
             bytes_accessed=pieces * piece * assets * 4,
@@ -146,7 +150,7 @@
         + lax.broadcasted_iota(jnp.int32, losses.shape, 1) * LANES
         + lax.broadcasted_iota(jnp.int32, losses.shape, 2)
     )
-    offsets = (ranks.astype(F32) - CENTER) / BAND
+    offsets = (ranks - CENTER) / BAND
     every = (place.astype(F32) - CENTER) / BAND
     kernel = jnp.exp(-0.5 * offsets * offsets) / total(jnp.exp(-0.5 * every * every))
     quantile = total(kernel * losses)
@@ -171,16 +175,25 @@
 def backward_kernel(order_ref, *refs):
     sums_ref, ranks_ref, tanh_ref, bend_ref, pnl_ref, turned_ref = refs[:6]
     conv_ref, hold_ref, desk_ref, price_ref = refs[6:10]
-    raw_ref, line_ref, last_ref, scaled, lines, wide, line_sums, both = refs[10:]
+    raw_ref, line_ref, last_ref, scaled, lines, wide, placed, both = refs[10:]
     step = pl.program_id(0)
     factors, scenarios = turned_ref.shape
-    desks = price_ref.shape[0]
+    desks = price_ref.shape[1]
     piece = scenarios // CLASSES
     cuts = piece // LANES
 
     @pl.when(step == 0)
     def _():
-        w, g = tail_of(sums_ref[:, 0:cuts, :], sums_ref[:, cuts : 2 * cuts, :], ranks_ref[...])
+        low = lax.broadcasted_iota(jnp.int32, (1, LANES), 1) < LANES // 2
+        for q in range(cuts):
+            for j in range(cuts):
+                here = ranks_ref[2 * j * cuts + q : 2 * j * cuts + q + 1, :].astype(F32)
+                there = ranks_ref[(2 * j + 1) * cuts + q : (2 * j + 1) * cuts + q + 1, :].astype(F32)
+                placed[2 * q, j : j + 1, :] = jnp.where(low, here, pltpu.roll(there, LANES // 2, 1))
+                placed[2 * q + 1, j : j + 1, :] = jnp.where(
+                    low, pltpu.roll(here, LANES // 2, 1), there
+                )
+        w, g = tail_of(sums_ref[:, 0:cuts, :], sums_ref[:, cuts : 2 * cuts, :], placed[...])
         both[:, 0:cuts, :] = w
         both[:, cuts : 2 * cuts, :] = g
         alloc = jnp.zeros((8, desks), F32)
@@ -222,9 +235,12 @@
 
     held = hold_ref[...]
     desk = lax.broadcasted_iota(jnp.int32, (desks, held.shape[1]), 0)
-    prices = jnp.sum(jnp.where(desk == desk_ref[...], price_ref[...], 0.0), axis=0, keepdims=True)
-    curved = dot_of(scaled[...], tanh_ref[...], ((1,), (0,)))
-    bent = dot_of(lines[...], bend_ref[...], ((1,), (0,)))
+    own = jnp.where(desk == desk_ref[...], 1.0, 0.0)
+    wide_price = jnp.broadcast_to(price_ref[...], (8, desks))
+    prices = dot_of(wide_price, own, ((1,), (0,)), lax.Precision.HIGHEST)[0:1, :]
+    part = pl.ds(pl.multiple_of(step * TILE, TILE), TILE)
+    curved = dot_of(scaled[...], tanh_ref[:, part], ((1,), (0,)))
+    bent = dot_of(lines[...], bend_ref[:, part], ((1,), (0,)))
     line = held * (prices * (bent[0:1, :] + bent[1:2, :]) + (bent[2:3, :] + bent[3:4, :]))
     raw = (conv_ref[...] * held) * (prices * curved[0:factors, :] + curved[factors:, :]) + held * (
         prices * wide[:, 0:1] + wide[:, 1:2]
@@ -242,7 +258,6 @@
     factors, desks = turned.shape[0], pnl.shape[1]
     whole = lambda *shape: pl.BlockSpec(shape, lambda i, o: (0,) * len(shape))
     line = pl.BlockSpec((1, TILE), lambda i, o: (0, i))
-    column = pl.BlockSpec((scenarios, TILE), lambda i, o: (0, i))
     return pl.pallas_call(
         backward_kernel,
         grid_spec=pltpu.PrefetchScalarGridSpec(
@@ -251,14 +266,14 @@
             in_specs=[
                 whole(*sums.shape),
                 whole(*ranks.shape),
-                column,
-                column,
+                whole(scenarios, assets),
+                whole(scenarios, assets),
                 whole(scenarios, desks),
                 whole(factors, scenarios),
                 line,
                 line,
                 line,
-                whole(desks, 1),
+                whole(1, desks),
             ],
             out_specs=(
                 pl.BlockSpec((TILE, factors), lambda i, o: (i, 0)),
@@ -269,7 +284,7 @@
                 pltpu.VMEM((2 * factors, scenarios), BF16),
                 pltpu.VMEM((8, scenarios), BF16),
                 pltpu.VMEM((factors, 2), F32),
-                pltpu.VMEM((8, LANES), F32),
+                pltpu.VMEM((CLASSES, sums.shape[1] // 2, LANES), F32),
                 pltpu.VMEM(sums.shape, F32),
             ],
         ),
@@ -278,7 +293,9 @@
             jax.ShapeDtypeStruct((1, assets), F32),
             jax.ShapeDtypeStruct((1, 2 * desks), F32),
         ),
-        compiler_params=pltpu.CompilerParams(dimension_semantics=("arbitrary",)),
+        compiler_params=pltpu.CompilerParams(
+            dimension_semantics=("arbitrary",), vmem_limit_bytes=BACKWARD_VMEM
+        ),
         cost_estimate=pl.CostEstimate(
             flops=4 * scenarios * assets * factors,
             bytes_accessed=scenarios * assets * 4,
@@ -307,8 +324,22 @@
             jax.ShapeDtypeStruct(raw.shape, F32),
             jax.ShapeDtypeStruct(line.shape, F32),
         ),
+        compiler_params=pltpu.CompilerParams(vmem_limit_bytes=SCALE_VMEM),
         name="scale",
     )(parts, raw, line)
+
+
+def summed_kernel(x_ref, out_ref):
+    out_ref[...] = jnp.broadcast_to(jnp.sum(x_ref[...], axis=0, keepdims=True), out_ref.shape)
+
+
+def summed_copies(x, copies):
+    return pl.pallas_call(
+        summed_kernel,
+        out_shape=jax.ShapeDtypeStruct((copies, *x.shape[1:]), F32),
+        compiler_params=pltpu.CompilerParams(vmem_limit_bytes=1 << 20),
+        name="summed_copies",
+    )(x)
 
 
 def for_each(x, axis):
@@ -346,12 +377,12 @@
     two = jnp.concatenate([two_up, two_down])
     held = forward([two, swap(two)], 6, held)
 
-    mine = jnp.sum(lax.all_to_all(held[4], CLOSE, 0, 0, tiled=True), axis=0)
-    mine = jnp.sum(for_each(mine, "far"), axis=0)
-    sums = for_each(mine, CLOSE)
-    placed = ranks.reshape(FAR, CLASSES, -1).transpose(1, 0, 2).reshape(CLASSES, -1, LANES)
+    mine = summed_copies(lax.all_to_all(held[4], CLOSE, 0, 0, tiled=True), FAR)
+    mine = summed_copies(lax.all_to_all(mine, "far", 0, 0, tiled=True), CLASSES)
+    sums = lax.all_to_all(mine, CLOSE, 0, 0, tiled=True)
+    placed = ranks.reshape(-1, LANES)
     raw, line, last = backward_call(
-        order, sums, placed, held[:4], *lines, desk_prices.reshape(-1, 1)
+        order, sums, placed, held[:4], *lines, desk_prices.reshape(1, -1)
     )
     entries = loadings.shape[0] * lax.axis_size(ASSET) * (loadings.shape[1] + 1)
     alloc, grad, conv = scale_call(for_each(last, ASSET), raw, line, entries)

time: 211 us -> 193 us (0.915)
  Pallas kernels: 44.7 us -> 28 us
  blocking collectives: 134 us -> 142 us
  waiting for transfers between devices: 5.36 us -> 1.53 us
  starting transfers between devices: 16.2 us -> 12.4 us
    all_to_all x1 -> x3, blocking collectives: 10.9 us -> 47.9 us  [the longest x1 28.9 us: shards(): mine = summed_copies(lax.all_to_all(mine, 'far', 0, 0, tiled=True), CLASSES)]
    all_to_all x3 -> x2, blocking collectives: 124 us -> 94.1 us  [for_each(): lax.all_to_all(jnp.broadcast_to(x, (lax.axis_size(axis), *x.shape)), axis...]
    pallas_call x3, Pallas kernels: 26.8 us -> 17.1 us  [forward_call(): pl.pallas_call(lambda *refs: forward_kernel(pieces, first, *refs), grid_s...]
    pallas_call x1, Pallas kernels: 15.5 us -> 9.76 us  [backward_call(): pl.pallas_call(backward_kernel, grid_spec=pltpu.PrefetchScalarGridSpec(nu...]
    all_to_all x1 -> x0, waiting for transfers between devices: 3.83 us -> none  [for_each(): lax.all_to_all(jnp.broadcast_to(x, (lax.axis_size(axis), *x.shape)), axis...]
    all_to_all x1 -> x0, starting transfers between devices: 3.72 us -> none  [for_each(): lax.all_to_all(jnp.broadcast_to(x, (lax.axis_size(axis), *x.shape)), axis...]
  transfers between devices with their start and end apart: 9 -> 8, of which waited for: 2 -> 1; matrix products, arithmetic and copies ran while one was open for 1% -> 0% of each run, Pallas kernels for 9% -> 7%
where the time goes in v2:
time: 193 us; the launch traced here: 192 us
  blocking collectives  142 us (74%)
  Pallas kernels  28 us (15%)
  starting transfers between devices  12.4 us (6%)
  local copies, waits for them, and re-layouts  5.84 us (3%)
    all_to_all x2, blocking collectives, for_each(): lax.all_to_all(jnp.broadcast_to(x, (lax.axis_size(axis), *x.shape)), axis...  94.1 us
    all_to_all x1, blocking collectives, shards(): mine = summed_copies(lax.all_to_all(mine, 'far', 0, 0, tiled=True), CLASSES)  28.9 us
    pallas_call x3, Pallas kernels, forward_call(): pl.pallas_call(lambda *refs: forward_kernel(pieces, first, *refs), grid_s...  17.1 us
    all_to_all x1, blocking collectives, shards(): mine = summed_copies(lax.all_to_all(held[4], CLOSE, 0, 0, tiled=True), FAR)  10.7 us
    pallas_call x1, Pallas kernels, backward_call(): pl.pallas_call(backward_kernel, grid_spec=pltpu.PrefetchScalarGridSpec(nu...  9.76 us
    all_to_all x1, blocking collectives, shards(): sums = lax.all_to_all(mine, CLOSE, 0, 0, tiled=True)  8.39 us
    ppermute x2, starting transfers between devices, shards(): from_up = lambda x: lax.ppermute(x, CHIPS, up)  6.47 us
    unnamed x25, local copies, waits for them, and re-layouts  5.74 us
  transfers between devices with their start and end apart: 8, of which 1 were waited for; matrix products, arithmetic and copies ran while one was open for 0% of the time, Pallas kernels for 7%

profile of v2, /device:TPU:38, one launch (start us, length us, event | category | flops | bytes accessed | tf_op | source)
XLA Modules:
  0.0 192.3 jit_solution(5154886949737864553)
XLA Ops:
  0.6 0.9 copy-done
  1.5 0.9 convolution_convert_fusion
  2.5 63.6 %all_to_all.25 = bf16[8,64,256]{2,1,0:T(8,128)(2,1)S(1)} all-to-all(bf16[8,64,256]{2,1,0:T(8,128)(2,1)S(1)} %broadcast_in_dim.6), channel_id=1, replica_groups=mesh['groups'=4,'far'=8,'near'=4,'core'=2] {'far'}, dimensions={0} | all-to-all | bytes 524288 | tf_op jit(solution)/shard_map/all_to_all | solution.py:346
  66.1 4.5 %collective-permute-start = (bf16[512,256]{1,0:T(8,128)(2,1)S(1)}, bf16[512,256]{1,0:T(8,128)(2,1)S(1)}, u32[]{:S(2)}, u32[]{:S(2)}) collective-permute-start(bf16[512,256]{1,0:T(8,128)(2,1)S(1)} %bitcast.12), channel_id=1, source_target_pairs={{0,62},{2,0},{4,2},{6,4},{8,6},{10,8},{12,10},{14,12},{16,14},{18,... | collective-permute-start | bytes 786440 | tf_op jit(solution)/shard_map/ppermute | solution.py:358
  70.5 4.9 %collective-permute-start.1 = (bf16[512,256]{1,0:T(8,128)(2,1)S(1)}, bf16[512,256]{1,0:T(8,128)(2,1)S(1)}, u32[]{:S(2)}, u32[]{:S(2)}) collective-permute-start(bf16[512,256]{1,0:T(8,128)(2,1)S(1)} %bitcast.13), channel_id=1, source_target_pairs={{0,2},{2,4},{4,6},{6,8},{8,10},{10,12},{12,14},{14,16},{16,18},{18... | collective-permute-start | bytes 786440 | tf_op jit(solution)/shard_map/ppermute | solution.py:359
  75.4 0.7 fusion.refs_0_.order_ref
  76.1 1.0 copy-done.1
  77.2 0.7 copy-done.3
  77.9 0.7 copy-done.5
  78.6 0.7 copy-done.7
  79.2 0.7 copy-done.10
  79.9 4.4 %forward_0.1 = (bf16[4096,1024]{1,0:T(8,128)(2,1)S(1)}, bf16[4096,1024]{1,0:T(8,128)(2,1)S(1)}, f32[4096,128]{1,0:T(8,128)S(1)}, bf16[256,4096]{1,0:T(8,128)(2,1)S(1)}, f32[8,8,128]{2,1,0:T(8,128)S(1)}) custom-call(s32[8]{0:T(128)S(1)} %fusion.refs_0_.order_ref, bf16[512,256]{1,0:T(8,128)(2,1)S(1)} %bitcast.14, ...), custom_call_target="tpu_custom_call" | custom-call | flops 805306368 | bytes 4194304 | tf_op jit(solution)/shard_map/forward_0/pallas_call | solution.py:114
  84.3 0.4 collective-permute-start.5
  85.0 2.0 %collective-permute-start.3 = (bf16[256,256]{1,0:T(8,128)(2,1)S(1)}, bf16[256,256]{1,0:T(8,128)(2,1)S(1)}, u32[]{:S(2)}, u32[]{:S(2)}) collective-permute-start(bf16[256,256]{1,0:T(8,128)(2,1)S(1)} %slice.6), channel_id=1, source_target_pairs={{0,62},{2,0},{4,2},{6,4},{8,6},{10,8},{12,10},{14,12},{16,14},{18,... | collective-permute-start | bytes 393224 | tf_op jit(solution)/shard_map/ppermute | solution.py:358
  87.3 1.0 copy-done.2
  88.3 8.2 %forward_2.1 = (bf16[4096,1024]{1,0:T(8,128)(2,1)S(1)}, bf16[4096,1024]{1,0:T(8,128)(2,1)S(1)}, f32[4096,128]{1,0:T(8,128)S(1)}, bf16[256,4096]{1,0:T(8,128)(2,1)S(1)}, f32[8,8,128]{2,1,0:T(8,128)S(1)}) custom-call(s32[8]{0:T(128)S(1)} %fusion.refs_0_.order_ref, ...), custom_call_target="tpu_custom_call", output_to_operand_aliasing={{0}: (10, {}), {1}: (11, {}), {2}: (12, {}), {3}: (13, {}),... | custom-call | flops 1610612736 | bytes 8388608 | tf_op jit(solution)/shard_map/forward_2/pallas_call | solution.py:114
  96.8 1.5 collective-permute-done.7.refs_2_
  98.3 4.4 %forward_6.1 = (bf16[4096,1024]{1,0:T(8,128)(2,1)S(1)}, bf16[4096,1024]{1,0:T(8,128)(2,1)S(1)}, f32[4096,128]{1,0:T(8,128)S(1)}, bf16[256,4096]{1,0:T(8,128)(2,1)S(1)}, f32[8,8,128]{2,1,0:T(8,128)S(1)}) custom-call(s32[8]{0:T(128)S(1)} %fusion.refs_0_.order_ref, ...), custom_call_target="tpu_custom_call", output_to_operand_aliasing={{0}: (8, {}), {1}: (9, {}), {2}: (10, {}), {3}: (11, {}), {... | custom-call | flops 805306368 | bytes 4194304 | tf_op jit(solution)/shard_map/forward_6/pallas_call | solution.py:114
  102.8 10.7 %all_to_all.26.x_ref = f32[8,8,128]{2,1,0:T(8,128)S(1)} all-to-all(f32[8,8,128]{2,1,0:T(8,128)S(1)} %get-tuple-element.62), channel_id=1, replica_groups=mesh['groups'=4,'far'=8,'near'=4,'core'=2] {'near','core'}, dimensions={0} | all-to-all | bytes 65536 | tf_op jit(solution)/shard_map/all_to_all | solution.py:380
  113.4 28.9 %all_to_all.27.x_ref = f32[8,8,128]{2,1,0:T(8,128)S(1)} all-to-all(f32[8,8,128]{2,1,0:T(8,128)S(1)} %summed_copies.2), channel_id=1, replica_groups=mesh['groups'=4,'far'=8,'near'=4,'core'=2] {'far'}, dimensions={0} | all-to-all | bytes 65536 | tf_op jit(solution)/shard_map/all_to_all | solution.py:381
  142.3 8.4 %all_to_all.28.refs_0_ = f32[8,8,128]{2,1,0:T(8,128)S(1)} all-to-all(f32[8,8,128]{2,1,0:T(8,128)S(1)} %summed_copies.3), channel_id=1, replica_groups=mesh['groups'=4,'far'=8,'near'=4,'core'=2] {'near','core'}, dimensions={0} | all-to-all | bytes 65536 | tf_op jit(solution)/shard_map/all_to_all | solution.py:382
  150.7 9.8 %backward.1 = (f32[1024,256]{1,0:T(8,128)S(1)}, f32[1,1024]{1,0:T(1,128)S(1)}, f32[1,256]{1,0:T(1,128)S(1)}) custom-call(s32[8]{0:T(128)S(1)} %fusion.refs_0_.order_ref, f32[8,8,128]{2,1,0:T(8,128)S(1)} %all_to_all.28.refs_0_, s32[32,128]{1,0:T(8,128)S(1)} %bitcast.27, bf16[4096,1024]{1,0:T(8,128)(2,1)S(1)} %get-tuple-element.63.refs_2_, ...), custom_call_target="tpu_custom_call" | custom-call | flops 4294967296 | bytes 16777216 | tf_op jit(solution)/shard_map/backward/pallas_call | solution.py:261
  160.5 30.5 %all_to_all.29.refs_0_ = f32[64,1,256]{2,1,0:T(1,128)S(1)} all-to-all(f32[64,1,256]{2,1,0:T(1,128)S(1)} %broadcast_in_dim.7), channel_id=1, replica_groups=mesh['groups'=4,'far'=8,'near'=4,'core'=2] {'far','near','core'}, dimensions={0} | all-to-all | bytes 131072 | tf_op jit(solution)/shard_map/all_to_all | solution.py:346
  191.1 1.2 scale.1
  (36 shorter events, 0.9 us)
Async XLA Ops:
  0.6 0.9 copy-start
  66.1 10.1 %collective-permute-start.2 = (bf16[512,256]{1,0:T(8,128)(2,1)S(1)}, bf16[512,256]{1,0:T(8,128)(2,1)S(1)}, u32[]{:S(2)}, u32[]{:S(2)}) collective-permute-start(bf16[512,256]{1,0:T(8,128)(2,1)S(1)} %bitcast.11), channel_id=1, source_target_pairs={{0,1},{1,0},{2,3},{3,2},{4,5},{5,4},{6,7},{7,6},{8,9},{9,8},{10,11... | collective-permute-start | bytes 786440 | tf_op jit(solution)/shard_map/ppermute | solution.py:357
  66.1 18.3 %collective-permute-start = (bf16[512,256]{1,0:T(8,128)(2,1)S(1)}, bf16[512,256]{1,0:T(8,128)(2,1)S(1)}, u32[]{:S(2)}, u32[]{:S(2)}) collective-permute-start(bf16[512,256]{1,0:T(8,128)(2,1)S(1)} %bitcast.12), channel_id=1, source_target_pairs={{0,62},{2,0},{4,2},{6,4},{8,6},{10,8},{12,10},{14,12},{16,14},{18,... | collective-permute-start | bytes 786440 | tf_op jit(solution)/shard_map/ppermute | solution.py:358
  70.5 13.8 %collective-permute-start.1 = (bf16[512,256]{1,0:T(8,128)(2,1)S(1)}, bf16[512,256]{1,0:T(8,128)(2,1)S(1)}, u32[]{:S(2)}, u32[]{:S(2)}) collective-permute-start(bf16[512,256]{1,0:T(8,128)(2,1)S(1)} %bitcast.13), channel_id=1, source_target_pairs={{0,2},{2,4},{4,6},{6,8},{8,10},{10,12},{12,14},{14,16},{16,18},{18... | collective-permute-start | bytes 786440 | tf_op jit(solution)/shard_map/ppermute | solution.py:359
  76.1 1.0 copy-start.1
  77.2 0.7 copy-start.3
  77.9 0.7 copy-start.5
  78.6 0.7 copy-start.7
  79.2 0.7 copy-start.10
  84.3 2.9 %collective-permute-start.5 = (bf16[512,256]{1,0:T(8,128)(2,1)S(1)}, bf16[512,256]{1,0:T(8,128)(2,1)S(1)}, u32[]{:S(2)}, u32[]{:S(2)}) collective-permute-start(bf16[512,256]{1,0:T(8,128)(2,1)S(1)} %collective-permute-done.refs_1_), channel_id=1, source_target_pairs={{0,1},{1,0},{2,3},{3,2},{4,5},{5,4},{6,7},{7,6},{8,9},{9,8},{10,11... | collective-permute-start | bytes 786440 | tf_op jit(solution)/shard_map/ppermute | solution.py:357
  84.7 2.6 %collective-permute-start.6 = (bf16[512,256]{1,0:T(8,128)(2,1)S(1)}, bf16[512,256]{1,0:T(8,128)(2,1)S(1)}, u32[]{:S(2)}, u32[]{:S(2)}) collective-permute-start(bf16[512,256]{1,0:T(8,128)(2,1)S(1)} %collective-permute-done.1.refs_2_), channel_id=1, source_target_pairs={{0,1},{1,0},{2,3},{3,2},{4,5},{5,4},{6,7},{7,6},{8,9},{9,8},{10,11... | collective-permute-start | bytes 786440 | tf_op jit(solution)/shard_map/ppermute | solution.py:357
  85.0 11.6 %collective-permute-start.3 = (bf16[256,256]{1,0:T(8,128)(2,1)S(1)}, bf16[256,256]{1,0:T(8,128)(2,1)S(1)}, u32[]{:S(2)}, u32[]{:S(2)}) collective-permute-start(bf16[256,256]{1,0:T(8,128)(2,1)S(1)} %slice.6), channel_id=1, source_target_pairs={{0,62},{2,0},{4,2},{6,4},{8,6},{10,8},{12,10},{14,12},{16,14},{18,... | collective-permute-start | bytes 393224 | tf_op jit(solution)/shard_map/ppermute | solution.py:358
  87.0 9.6 %collective-permute-start.4 = (bf16[256,256]{1,0:T(8,128)(2,1)S(1)}, bf16[256,256]{1,0:T(8,128)(2,1)S(1)}, u32[]{:S(2)}, u32[]{:S(2)}) collective-permute-start(bf16[256,256]{1,0:T(8,128)(2,1)S(1)} %slice.7), channel_id=1, source_target_pairs={{0,2},{2,4},{4,6},{6,8},{8,10},{10,12},{12,14},{14,16},{16,18},{18... | collective-permute-start | bytes 393224 | tf_op jit(solution)/shard_map/ppermute | solution.py:359
  87.3 1.0 copy-start.2
  96.6 54.1 %copy-start.4 = (f32[1024]{0:T(1024)S(1)}, f32[1024]{0:T(1024)}, u32[]{:S(2)}) copy-start(f32[1024]{0:T(1024)} %param.13) | copy-start | bytes 12292
  96.6 54.1 %copy-start.6 = (f32[1024]{0:T(1024)S(1)}, f32[1024]{0:T(1024)}, u32[]{:S(2)}) copy-start(f32[1024]{0:T(1024)} %param.14) | copy-start | bytes 12292
  96.7 54.1 %copy-start.8 = (s32[1024]{0:T(1024)S(1)}, s32[1024]{0:T(1024)}, u32[]{:S(2)}) copy-start(s32[1024]{0:T(1024)} %param.15) | copy-start | bytes 12292
  96.7 54.0 %copy-start.9 = (s32[4096]{0:T(1024)S(1)}, s32[4096]{0:T(1024)}, u32[]{:S(2)}) copy-start(s32[4096]{0:T(1024)} %param.16) | copy-start | bytes 49156
  96.7 54.0 %copy-start.11 = (f32[128]{0:T(128)S(1)}, f32[128]{0:T(128)}, u32[]{:S(2)}) copy-start(f32[128]{0:T(128)} %param.17) | copy-start | bytes 1540
  96.7 1.7 collective-permute-start.7

commit v3 on v2

--- a/solution.py
+++ b/solution.py
@@ -23,6 +23,7 @@
 BF16 = jnp.bfloat16
 LANES = 128
 TILE = 256
+PREPARE_VMEM = 65_900_000
 FORWARD_VMEM = 16 << 20
 BACKWARD_VMEM = 20 << 20
 SCALE_VMEM = 8 << 20
@@ -34,22 +35,76 @@
     return lax.dot_general(a, b, (dims, ((), ())), precision=precision, preferred_element_type=F32)
 
 
+def prepare_kernel(*refs):
+    given, refs = refs[:6], refs[6:]
+    copies_ref, table_ref, asset_ref = refs[:3]
+    draws, mix, conv, hold, desk, price, sems = refs[3:]
+    moves = [
+        pltpu.make_async_copy(source, target, sems.at[i])
+        for i, (source, target) in enumerate(
+            zip(given, (draws, mix, desk, price, conv, hold))
+        )
+    ]
+    for move in moves:
+        move.start()
+    for move in moves[:2]:
+        move.wait()
+    local = dot_of(draws[...], mix[...], ((1,), (0,))).astype(BF16)
+    copies_ref[...] = jnp.broadcast_to(local[None], copies_ref.shape)
+    for move in moves[2:]:
+        move.wait()
+    desks, assets = table_ref.shape
+    place = lax.broadcasted_iota(jnp.int32, (desks, assets), 0)
+    own = jnp.where(place == desk[...], 1.0, 0.0)
+    table_ref[...] = own.astype(BF16)
+    wide = jnp.broadcast_to(price[...], (8, desks))
+    asset_ref[0:1, :] = conv[...]
+    asset_ref[1:2, :] = hold[...]
+    asset_ref[2:3, :] = dot_of(wide, own, ((1,), (0,)), lax.Precision.HIGHEST)[0:1, :]
+    asset_ref[3:4, 0:desks] = price[...]
+
+
+def prepare_call(scen_draws, factor_mix, desk_map, prices, convexity, holdings):
+    assets, desks = desk_map.shape[1], prices.shape[1]
+    hbm = pl.BlockSpec(memory_space=pltpu.HBM)
+    vmem = pl.BlockSpec(memory_space=pltpu.VMEM)
+    row = pltpu.VMEM((1, assets), F32)
+    return pl.pallas_call(
+        prepare_kernel,
+        in_specs=[hbm] * 6,
+        out_specs=(vmem,) * 3,
+        out_shape=(
+            jax.ShapeDtypeStruct((FAR, *scen_draws.shape), BF16),
+            jax.ShapeDtypeStruct((desks, assets), BF16),
+            jax.ShapeDtypeStruct((8, assets), F32),
+        ),
+        scratch_shapes=[
+            pltpu.VMEM(scen_draws.shape, BF16),
+            pltpu.VMEM(factor_mix.shape, BF16),
+            row,
+            row,
+            pltpu.VMEM((1, assets), jnp.int32),
+            pltpu.VMEM((1, desks), F32),
+            pltpu.SemaphoreType.DMA((6,)),
+        ],
+        compiler_params=pltpu.CompilerParams(vmem_limit_bytes=PREPARE_VMEM),
+        name="prepare",
+    )(scen_draws, factor_mix, desk_map, prices, convexity, holdings)
+
+
 def forward_kernel(pieces, first, order_ref, *refs):
     shock_refs, refs = refs[:pieces], refs[pieces:]
-    load_ref, conv_ref, hold_ref, desk_ref, price_ref = refs[:5]
-    outs = refs[5:] if first else refs[10:]
-    tanh_ref, bend_ref, pnl_ref, turned_ref, sums_ref, rows, table = outs
+    load_ref, table, asset_ref = refs[:3]
+    outs = refs[3:] if first else refs[8:]
+    tanh_ref, bend_ref, pnl_ref, turned_ref, sums_ref, rows = outs
     step = pl.program_id(0)
     piece = shock_refs[0].shape[0]
-    assets = load_ref.shape[0]
-    desks = price_ref.shape[1]
+    desks, assets = table.shape
 
     @pl.when(step == 0)
     def _():
         for i in range(pieces):
             rows[i * piece : (i + 1) * piece, :] = shock_refs[i][...]
-        desk = lax.broadcasted_iota(jnp.int32, (desks, assets), 0)
-        table[...] = jnp.where(desk == desk_ref[...], 1.0, 0.0).astype(BF16)
 
     size = tanh_ref.shape[0]
     shocks = rows[pl.ds(pl.multiple_of(step * size, size), size), :]
@@ -60,13 +115,13 @@
         exposure = dot_of(shocks, load_ref[part, :], ((1,), (1,)))
         size_of = jnp.abs(exposure)
         bend = size_of + (jnp.log(1.0 + jnp.exp(-2.0 * size_of)) - LOG2)
-        held = hold_ref[:, part] * (exposure + conv_ref[:, part] * bend)
+        held = asset_ref[1:2, part] * (exposure + asset_ref[0:1, part] * bend)
         tanh_ref[:, part] = jnp.tanh(exposure).astype(BF16)
         bend_ref[:, part] = bend.astype(BF16)
         pnl = pnl + dot_of(held.astype(BF16), table[:, part], ((1,), (1,)))
     pnl_ref[...] = pnl
     row = lax.broadcasted_iota(jnp.int32, (8, desks), 0)
-    weigh = jnp.where(row == 0, -1.0, jnp.where(row == 1, price_ref[...], 0.0))
+    weigh = jnp.where(row == 0, -1.0, jnp.where(row == 1, asset_ref[3:4, 0:desks], 0.0))
     sums = dot_of(weigh, pnl, ((1,), (1,)), lax.Precision.HIGHEST)
     lines = size // LANES
     for part in range(2):
@@ -76,10 +131,10 @@
             ]
 
 
-def forward_call(shocks, place, order, loadings, convexity, holdings, desk_map, prices, held):
+def forward_call(shocks, place, order, loadings, table, lines, held):
     pieces, piece, factors = len(shocks), *shocks[0].shape
     scenarios = piece * CLASSES
-    assets, desks = loadings.shape[0], prices.shape[1]
+    desks, assets = table.shape
     size = piece
     first = held is None
     base = place
@@ -100,12 +155,10 @@
     )
     in_specs = [whole((piece, factors))] * pieces + [
         whole((assets, factors)),
-        whole((1, assets)),
-        whole((1, assets)),
-        whole((1, assets)),
-        whole((1, desks)),
+        whole((desks, assets)),
+        whole((8, assets)),
     ]
-    operands = [*shocks, loadings, convexity, holdings, desk_map, prices]
+    operands = [*shocks, loadings, table, lines]
     aliases = {}
     if not first:
         aliases = {1 + len(operands) + i: i for i in range(5)}
@@ -120,7 +173,6 @@
             out_specs=out_specs,
             scratch_shapes=[
                 pltpu.VMEM((pieces * piece, factors), BF16),
-                pltpu.VMEM((desks, assets), BF16),
             ],
         ),
         out_shape=out_shape,
@@ -174,11 +226,11 @@
 
 def backward_kernel(order_ref, *refs):
     sums_ref, ranks_ref, tanh_ref, bend_ref, pnl_ref, turned_ref = refs[:6]
-    conv_ref, hold_ref, desk_ref, price_ref = refs[6:10]
-    raw_ref, line_ref, last_ref, scaled, lines, wide, placed, both = refs[10:]
+    asset_ref = refs[6]
+    raw_ref, line_ref, last_ref, scaled, lines, wide, placed, both = refs[7:]
     step = pl.program_id(0)
     factors, scenarios = turned_ref.shape
-    desks = price_ref.shape[1]
+    desks = pnl_ref.shape[1]
     piece = scenarios // CLASSES
     cuts = piece // LANES
 
@@ -233,16 +285,12 @@
         last_ref[:, 0:desks] = alloc[0:1, :] / scenarios
         last_ref[:, desks : 2 * desks] = jnp.zeros((1, desks), F32)
 
-    held = hold_ref[...]
-    desk = lax.broadcasted_iota(jnp.int32, (desks, held.shape[1]), 0)
-    own = jnp.where(desk == desk_ref[...], 1.0, 0.0)
-    wide_price = jnp.broadcast_to(price_ref[...], (8, desks))
-    prices = dot_of(wide_price, own, ((1,), (0,)), lax.Precision.HIGHEST)[0:1, :]
     part = pl.ds(pl.multiple_of(step * TILE, TILE), TILE)
+    conv, held, prices = asset_ref[0:1, part], asset_ref[1:2, part], asset_ref[2:3, part]
     curved = dot_of(scaled[...], tanh_ref[:, part], ((1,), (0,)))
     bent = dot_of(lines[...], bend_ref[:, part], ((1,), (0,)))
     line = held * (prices * (bent[0:1, :] + bent[1:2, :]) + (bent[2:3, :] + bent[3:4, :]))
-    raw = (conv_ref[...] * held) * (prices * curved[0:factors, :] + curved[factors:, :]) + held * (
+    raw = (conv * held) * (prices * curved[0:factors, :] + curved[factors:, :]) + held * (
         prices * wide[:, 0:1] + wide[:, 1:2]
     )
     raw_ref[...] = raw.T
@@ -252,7 +300,7 @@
         last_ref[:, desks : 2 * desks] += squares[:, low : low + desks]
 
 
-def backward_call(order, sums, ranks, held, convexity, holdings, desk_map, prices):
+def backward_call(order, sums, ranks, held, lines):
     tanh, bend, pnl, turned = held
     scenarios, assets = tanh.shape
     factors, desks = turned.shape[0], pnl.shape[1]
@@ -270,10 +318,7 @@
                 whole(scenarios, assets),
                 whole(scenarios, desks),
                 whole(factors, scenarios),
-                line,
-                line,
-                line,
-                whole(1, desks),
+                whole(8, assets),
             ],
             out_specs=(
                 pl.BlockSpec((TILE, factors), lambda i, o: (i, 0)),
@@ -302,7 +347,7 @@
             transcendentals=0,
         ),
         name="backward",
-    )(order, sums, ranks, tanh, bend, pnl, turned, convexity, holdings, desk_map, prices)
+    )(order, sums, ranks, tanh, bend, pnl, turned, lines)
 
 
 def scale_kernel(entries, parts_ref, raw_ref, line_ref, alloc_ref, grad_ref, conv_ref):
@@ -358,12 +403,19 @@
     from_up = lambda x: lax.ppermute(x, CHIPS, up)
     from_down = lambda x: lax.ppermute(x, CHIPS, down)
 
-    local = jnp.dot(scen_draws, factor_mix, preferred_element_type=F32).astype(BF16)
-    own = for_each(local, "far").reshape(-1, local.shape[1])
+    order, scen_draws = lax.optimization_barrier((order, scen_draws))
+    copies, table, lines = prepare_call(
+        scen_draws,
+        factor_mix,
+        desk_map.reshape(1, -1),
+        desk_prices.reshape(1, -1),
+        convexity.reshape(1, -1),
+        holdings.reshape(1, -1),
+    )
+    own = lax.all_to_all(copies, "far", 0, 0, tiled=True).reshape(-1, copies.shape[2])
     half = own.shape[0] // 2
-    lines = [x.reshape(1, -1) for x in (convexity, holdings, desk_map)]
     forward = lambda shocks, place, held: forward_call(
-        shocks, place, order, loadings, *lines, desk_prices.reshape(1, -1), held
+        shocks, place, order, loadings, table, lines, held
     )
     next_up, next_down = from_up(own), from_down(own)
     own_other = swap(own)
@@ -375,17 +427,18 @@
     held = forward([next_up, next_down, up_other, down_other], 2, held)
     two_up, two_down, held = lax.optimization_barrier((two_up, two_down, held))
     two = jnp.concatenate([two_up, two_down])
-    held = forward([two, swap(two)], 6, held)
+    two_other = swap(two)
+    held = forward([two], 6, held)
+    two_other, held = lax.optimization_barrier((two_other, held))
+    held = forward([two_other], 7, held)
 
     mine = summed_copies(lax.all_to_all(held[4], CLOSE, 0, 0, tiled=True), FAR)
     mine = summed_copies(lax.all_to_all(mine, "far", 0, 0, tiled=True), CLASSES)
     sums = lax.all_to_all(mine, CLOSE, 0, 0, tiled=True)
     placed = ranks.reshape(-1, LANES)
-    raw, line, last = backward_call(
-        order, sums, placed, held[:4], *lines, desk_prices.reshape(1, -1)
-    )
+    raw, line, last = backward_call(order, sums, placed, held[:4], lines)
     entries = loadings.shape[0] * lax.axis_size(ASSET) * (loadings.shape[1] + 1)
-    alloc, grad, conv = scale_call(for_each(last, ASSET), raw, line, entries)
+    alloc, grad, conv = scale_call(for_each(last + swap(last), CHIPS), raw, line, entries)
     return (alloc.reshape(-1), grad, conv.reshape(-1))
 
 

time: 193 us -> 188 us (0.974)
  blocking collectives: 142 us -> 137 us
  local copies, waits for them, and re-layouts: 5.84 us -> 2.82 us
  Pallas kernels: 28 us -> 30.4 us
    all_to_all x2 -> x1, blocking collectives: 94.1 us -> 26.8 us  [for_each(): lax.all_to_all(jnp.broadcast_to(x, (lax.axis_size(axis), *x.shape)), axis...]
    all_to_all x0 -> x1, blocking collectives: none -> 63.8 us  [shards(): lax.all_to_all(copies, 'far', 0, 0, tiled=True).reshape(-1, copies.shape[2])]
    unnamed x25 -> x11, local copies, waits for them, and re-layouts: 5.74 us -> 2.77 us
    pallas_call x0 -> x1, Pallas kernels: none -> 2.19 us  [prepare_call(): pl.pallas_call(prepare_kernel, in_specs=[hbm] * 6, out_specs=(vmem,) * 3,...]
    pallas_call x3 -> x4, Pallas kernels: 17.1 us -> 17.3 us  [forward_call(): pl.pallas_call(lambda *refs: forward_kernel(pieces, first, *refs), grid_s...]
  transfers between devices with their start and end apart: 8 -> 9, of which waited for: 1 -> 2; matrix products, arithmetic and copies ran while one was open for 0% -> 0% of each run, Pallas kernels for 7% -> 8%
where the time goes in v3:
time: 188 us; the launch traced here: 187 us
  blocking collectives  137 us (73%)
  Pallas kernels  30.4 us (16%)
  starting transfers between devices  12.5 us (7%)
  local copies, waits for them, and re-layouts  2.82 us (2%)
  waiting for transfers between devices  2.62 us (1%)
    all_to_all x1, blocking collectives, shards(): lax.all_to_all(copies, 'far', 0, 0, tiled=True).reshape(-1, copies.shape[2])  63.8 us
    all_to_all x1, blocking collectives, shards(): mine = summed_copies(lax.all_to_all(mine, 'far', 0, 0, tiled=True), CLASSES)  27.7 us
    all_to_all x1, blocking collectives, for_each(): lax.all_to_all(jnp.broadcast_to(x, (lax.axis_size(axis), *x.shape)), axis...  26.8 us
    pallas_call x4, Pallas kernels, forward_call(): pl.pallas_call(lambda *refs: forward_kernel(pieces, first, *refs), grid_s...  17.3 us
    all_to_all x1, blocking collectives, shards(): mine = summed_copies(lax.all_to_all(held[4], CLOSE, 0, 0, tiled=True), FAR)  10.7 us
    pallas_call x1, Pallas kernels, backward_call(): pl.pallas_call(backward_kernel, grid_spec=pltpu.PrefetchScalarGridSpec(nu...  9.72 us
    all_to_all x1, blocking collectives, shards(): sums = lax.all_to_all(mine, CLOSE, 0, 0, tiled=True)  8.32 us
    ppermute x2, starting transfers between devices, shards(): from_up = lambda x: lax.ppermute(x, CHIPS, up)  6.31 us
  transfers between devices with their start and end apart: 9, of which 2 were waited for; matrix products, arithmetic and copies ran while one was open for 0% of the time, Pallas kernels for 8%

profile of v3, /device:TPU:38, one launch (start us, length us, event | category | flops | bytes accessed | tf_op | source)
XLA Modules:
  0.0 187.1 jit_solution(10508958094592188512)
XLA Ops:
  0.6 0.7 fusion.refs_0_.order_ref
  1.3 2.2 %prepare.1 = (bf16[8,64,256]{2,1,0:T(8,128)(2,1)}, bf16[128,1024]{1,0:T(8,128)(2,1)}, f32[8,1024]{1,0:T(8,128)}) custom-call(bf16[64,256]{1,0:T(8,128)(2,1)} %refs_0_, bf16[256,256]{1,0:T(8,128)(2,1)} %refs_1_.1, s32[1,1024]{1,0:T(1,128)} %bitcast.14, f32[1,128]{1,0:T(1,128)} %bitcast.18, f32[1,1024]{1,0:T(1,128)} %bitcast.15, f32[1,1024]{1,0:T(1,128)} %bitcast.16), custom_call_target="tpu_custom_call" | custom-call | tf_op jit(solution)/shard_map/prepare/pallas_call | solution.py:72
  3.5 63.8 %all_to_all.25 = bf16[8,64,256]{2,1,0:T(8,128)(2,1)S(1)} all-to-all(bf16[8,64,256]{2,1,0:T(8,128)(2,1)} %get-tuple-element.56), channel_id=1, replica_groups=mesh['groups'=4,'far'=8,'near'=4,'core'=2] {'far'}, dimensions={0} | all-to-all | bytes 524288 | tf_op jit(solution)/shard_map/all_to_all | solution.py:415
  67.3 4.5 %collective-permute-start = (bf16[512,256]{1,0:T(8,128)(2,1)S(1)}, bf16[512,256]{1,0:T(8,128)(2,1)S(1)}, u32[]{:S(2)}, u32[]{:S(2)}) collective-permute-start(bf16[512,256]{1,0:T(8,128)(2,1)S(1)} %bitcast.10), channel_id=1, source_target_pairs={{0,62},{2,0},{4,2},{6,4},{8,6},{10,8},{12,10},{14,12},{16,14},{18,... | collective-permute-start | bytes 786440 | tf_op jit(solution)/shard_map/ppermute | solution.py:403
  71.8 4.9 %collective-permute-start.1 = (bf16[512,256]{1,0:T(8,128)(2,1)S(1)}, bf16[512,256]{1,0:T(8,128)(2,1)S(1)}, u32[]{:S(2)}, u32[]{:S(2)}) collective-permute-start(bf16[512,256]{1,0:T(8,128)(2,1)S(1)} %bitcast.11), channel_id=1, source_target_pairs={{0,2},{2,4},{4,6},{6,8},{8,10},{10,12},{12,14},{14,16},{16,18},{18... | collective-permute-start | bytes 786440 | tf_op jit(solution)/shard_map/ppermute | solution.py:404
  76.7 1.0 copy-done
  77.7 0.9 copy-done.1
  78.7 0.8 copy-done.2
  79.5 4.4 %forward_0.1 = (bf16[4096,1024]{1,0:T(8,128)(2,1)S(1)}, bf16[4096,1024]{1,0:T(8,128)(2,1)S(1)}, f32[4096,128]{1,0:T(8,128)S(1)}, bf16[256,4096]{1,0:T(8,128)(2,1)S(1)}, f32[8,8,128]{2,1,0:T(8,128)S(1)}) custom-call(s32[8]{0:T(128)S(1)} %fusion.refs_0_.order_ref, bf16[512,256]{1,0:T(8,128)(2,1)S(1)} %bitcast.12, ...), custom_call_target="tpu_custom_call" | custom-call | flops 805306368 | bytes 4194304 | tf_op jit(solution)/shard_map/forward_0/pallas_call | solution.py:167
  83.8 1.5 collective-permute-done.1.refs_2_
  85.3 0.5 collective-permute-start.6
  85.8 1.9 collective-permute-start.3
  87.7 0.3 collective-permute-start.4
  88.0 8.2 %forward_2.1 = (bf16[4096,1024]{1,0:T(8,128)(2,1)S(1)}, bf16[4096,1024]{1,0:T(8,128)(2,1)S(1)}, f32[4096,128]{1,0:T(8,128)S(1)}, bf16[256,4096]{1,0:T(8,128)(2,1)S(1)}, f32[8,8,128]{2,1,0:T(8,128)S(1)}) custom-call(s32[8]{0:T(128)S(1)} %fusion.refs_0_.order_ref, ...), custom_call_target="tpu_custom_call", output_to_operand_aliasing={{0}: (8, {}), {1}: (9, {}), {2}: (10, {}), {3}: (11, {}), {... | custom-call | flops 1610612736 | bytes 8388608 | tf_op jit(solution)/shard_map/forward_2/pallas_call | solution.py:167
  96.2 0.3 collective-permute-start.7
  96.5 2.4 %forward_6.1 = (bf16[4096,1024]{1,0:T(8,128)(2,1)S(1)}, bf16[4096,1024]{1,0:T(8,128)(2,1)S(1)}, f32[4096,128]{1,0:T(8,128)S(1)}, bf16[256,4096]{1,0:T(8,128)(2,1)S(1)}, f32[8,8,128]{2,1,0:T(8,128)S(1)}) custom-call(s32[8]{0:T(128)S(1)} %fusion.refs_0_.order_ref, ...), custom_call_target="tpu_custom_call", output_to_operand_aliasing={{0}: (5, {}), {1}: (6, {}), {2}: (7, {}), {3}: (8, {}), {4}... | custom-call | flops 402653184 | bytes 2097152 | tf_op jit(solution)/shard_map/forward_6/pallas_call | solution.py:167
  98.9 2.4 %forward_7.1 = (bf16[4096,1024]{1,0:T(8,128)(2,1)S(1)}, bf16[4096,1024]{1,0:T(8,128)(2,1)S(1)}, f32[4096,128]{1,0:T(8,128)S(1)}, bf16[256,4096]{1,0:T(8,128)(2,1)S(1)}, f32[8,8,128]{2,1,0:T(8,128)S(1)}) custom-call(s32[8]{0:T(128)S(1)} %fusion.refs_0_.order_ref, ...), custom_call_target="tpu_custom_call", output_to_operand_aliasing={{0}: (5, {}), {1}: (6, {}), {2}: (7, {}), {3}: (8, {}), {4}... | custom-call | flops 402653184 | bytes 2097152 | tf_op jit(solution)/shard_map/forward_7/pallas_call | solution.py:167
  101.3 10.7 %all_to_all.26.x_ref = f32[8,8,128]{2,1,0:T(8,128)S(1)} all-to-all(f32[8,8,128]{2,1,0:T(8,128)S(1)} %get-tuple-element.94), channel_id=1, replica_groups=mesh['groups'=4,'far'=8,'near'=4,'core'=2] {'near','core'}, dimensions={0} | all-to-all | bytes 65536 | tf_op jit(solution)/shard_map/all_to_all | solution.py:435
  112.0 27.7 %all_to_all.27.x_ref = f32[8,8,128]{2,1,0:T(8,128)S(1)} all-to-all(f32[8,8,128]{2,1,0:T(8,128)S(1)} %summed_copies.2), channel_id=1, replica_groups=mesh['groups'=4,'far'=8,'near'=4,'core'=2] {'far'}, dimensions={0} | all-to-all | bytes 65536 | tf_op jit(solution)/shard_map/all_to_all | solution.py:436
  139.7 8.3 %all_to_all.28.refs_0_ = f32[8,8,128]{2,1,0:T(8,128)S(1)} all-to-all(f32[8,8,128]{2,1,0:T(8,128)S(1)} %summed_copies.3), channel_id=1, replica_groups=mesh['groups'=4,'far'=8,'near'=4,'core'=2] {'near','core'}, dimensions={0} | all-to-all | bytes 65536 | tf_op jit(solution)/shard_map/all_to_all | solution.py:437
  148.1 9.7 %backward.1 = (f32[1024,256]{1,0:T(8,128)S(1)}, f32[1,1024]{1,0:T(1,128)S(1)}, f32[1,256]{1,0:T(1,128)S(1)}) custom-call(s32[8]{0:T(128)S(1)} %fusion.refs_0_.order_ref, f32[8,8,128]{2,1,0:T(8,128)S(1)} %all_to_all.28.refs_0_, s32[32,128]{1,0:T(8,128)S(1)} %bitcast.13, bf16[4096,1024]{1,0:T(8,128)(2,1)S(1)} %get-tuple-element.95.refs_2_, ...), custom_call_target="tpu_custom_call" | custom-call | flops 4294967296 | bytes 16777216 | tf_op jit(solution)/shard_map/backward/pallas_call | solution.py:309
  157.9 1.1 collective-permute-done.8
  159.1 26.8 %all_to_all.29.refs_0_ = f32[32,1,256]{2,1,0:T(1,128)S(1)} all-to-all(f32[32,1,256]{2,1,0:T(1,128)S(1)} %broadcast_in_dim.3), channel_id=1, replica_groups=mesh['groups'=4,'far'=8,'near'=4,'core'=2] {'far','near'}, dimensions={0} | all-to-all | bytes 65536 | tf_op jit(solution)/shard_map/all_to_all | solution.py:391
  185.9 1.2 scale.1
  (25 shorter events, 0.3 us)
Async XLA Ops:
  67.3 9.4 %collective-permute-start.2 = (bf16[512,256]{1,0:T(8,128)(2,1)S(1)}, bf16[512,256]{1,0:T(8,128)(2,1)S(1)}, u32[]{:S(2)}, u32[]{:S(2)}) collective-permute-start(bf16[512,256]{1,0:T(8,128)(2,1)S(1)} %bitcast.9), channel_id=1, source_target_pairs={{0,1},{1,0},{2,3},{3,2},{4,5},{5,4},{6,7},{7,6},{8,9},{9,8},{10,11... | collective-permute-start | bytes 786440 | tf_op jit(solution)/shard_map/ppermute | solution.py:402
  67.3 16.5 %collective-permute-start = (bf16[512,256]{1,0:T(8,128)(2,1)S(1)}, bf16[512,256]{1,0:T(8,128)(2,1)S(1)}, u32[]{:S(2)}, u32[]{:S(2)}) collective-permute-start(bf16[512,256]{1,0:T(8,128)(2,1)S(1)} %bitcast.10), channel_id=1, source_target_pairs={{0,62},{2,0},{4,2},{6,4},{8,6},{10,8},{12,10},{14,12},{16,14},{18,... | collective-permute-start | bytes 786440 | tf_op jit(solution)/shard_map/ppermute | solution.py:403
  71.8 13.5 %collective-permute-start.1 = (bf16[512,256]{1,0:T(8,128)(2,1)S(1)}, bf16[512,256]{1,0:T(8,128)(2,1)S(1)}, u32[]{:S(2)}, u32[]{:S(2)}) collective-permute-start(bf16[512,256]{1,0:T(8,128)(2,1)S(1)} %bitcast.11), channel_id=1, source_target_pairs={{0,2},{2,4},{4,6},{6,8},{8,10},{10,12},{12,14},{14,16},{16,18},{18... | collective-permute-start | bytes 786440 | tf_op jit(solution)/shard_map/ppermute | solution.py:404
  76.7 1.0 copy-start
  77.7 0.9 copy-start.1
  78.7 0.8 copy-start.2
  85.3 2.7 %collective-permute-start.5 = (bf16[512,256]{1,0:T(8,128)(2,1)S(1)}, bf16[512,256]{1,0:T(8,128)(2,1)S(1)}, u32[]{:S(2)}, u32[]{:S(2)}) collective-permute-start(bf16[512,256]{1,0:T(8,128)(2,1)S(1)} %collective-permute-done.refs_1_), channel_id=1, source_target_pairs={{0,1},{1,0},{2,3},{3,2},{4,5},{5,4},{6,7},{7,6},{8,9},{9,8},{10,11... | collective-permute-start | bytes 786440 | tf_op jit(solution)/shard_map/ppermute | solution.py:402
  85.3 2.7 %collective-permute-start.6 = (bf16[512,256]{1,0:T(8,128)(2,1)S(1)}, bf16[512,256]{1,0:T(8,128)(2,1)S(1)}, u32[]{:S(2)}, u32[]{:S(2)}) collective-permute-start(bf16[512,256]{1,0:T(8,128)(2,1)S(1)} %collective-permute-done.1.refs_2_), channel_id=1, source_target_pairs={{0,1},{1,0},{2,3},{3,2},{4,5},{5,4},{6,7},{7,6},{8,9},{9,8},{10,11... | collective-permute-start | bytes 786440 | tf_op jit(solution)/shard_map/ppermute | solution.py:402
  85.8 10.3 %collective-permute-start.3 = (bf16[256,256]{1,0:T(8,128)(2,1)S(1)}, bf16[256,256]{1,0:T(8,128)(2,1)S(1)}, u32[]{:S(2)}, u32[]{:S(2)}) collective-permute-start(bf16[256,256]{1,0:T(8,128)(2,1)S(1)} %slice.6), channel_id=1, source_target_pairs={{0,62},{2,0},{4,2},{6,4},{8,6},{10,8},{12,10},{14,12},{16,14},{18,... | collective-permute-start | bytes 393224 | tf_op jit(solution)/shard_map/ppermute | solution.py:403
  87.7 8.5 %collective-permute-start.4 = (bf16[256,256]{1,0:T(8,128)(2,1)S(1)}, bf16[256,256]{1,0:T(8,128)(2,1)S(1)}, u32[]{:S(2)}, u32[]{:S(2)}) collective-permute-start(bf16[256,256]{1,0:T(8,128)(2,1)S(1)} %slice.7), channel_id=1, source_target_pairs={{0,2},{2,4},{4,6},{6,8},{8,10},{10,12},{12,14},{14,16},{16,18},{18... | collective-permute-start | bytes 393224 | tf_op jit(solution)/shard_map/ppermute | solution.py:404
  96.2 2.7 %collective-permute-start.7 = (bf16[512,256]{1,0:T(8,128)(2,1)S(1)}, bf16[512,256]{1,0:T(8,128)(2,1)S(1)}, u32[]{:S(2)}, u32[]{:S(2)}) collective-permute-start(bf16[512,256]{1,0:T(8,128)(2,1)S(1)} %constant_dynamic-update-slice_fusion.refs_1_), channel_id=1, source_target_pairs={{0,1},{1,0},{2,3},{3,2},{4,5},{5,4},{6,7},{7,6},{8,9},{9,8},{10,11... | collective-permute-start | bytes 786440 | tf_op jit(solution)/shard_map/ppermute | solution.py:402
  98.9 49.1 %copy-start.3 = (f32[8,1024]{1,0:T(8,128)S(1)}, f32[8,1024]{1,0:T(8,128)}, u32[]{:S(2)}) copy-start(f32[8,1024]{1,0:T(8,128)} %get-tuple-element.58.refs_5_.refs_7_.refs_4_.refs_6_) | copy-start | bytes 98308
  98.9 49.1 %copy-start.4 = (s32[4096]{0:T(1024)S(1)}, s32[4096]{0:T(1024)}, u32[]{:S(2)}) copy-start(s32[4096]{0:T(1024)} %param.16) | copy-start | bytes 49156
  157.8 1.3 collective-permute-start.8

commit v4 on v3

--- a/solution.py
+++ b/solution.py
@@ -396,14 +396,12 @@
 def shards(scen_draws, factor_mix, loadings, convexity, holdings, desk_map, ranks, desk_prices):
     chips = FAR * NEAR
     near, core = lax.axis_index("near"), lax.axis_index("core")
-    order = ((near + STEPS_Z) % NEAR) * 2 + (core + OTHER) % 2
     up = [(i, (i - 1) % chips) for i in range(chips)]
     down = [(i, (i + 1) % chips) for i in range(chips)]
     swap = lambda x: lax.ppermute(x, "core", [(0, 1), (1, 0)])
     from_up = lambda x: lax.ppermute(x, CHIPS, up)
     from_down = lambda x: lax.ppermute(x, CHIPS, down)
 
-    order, scen_draws = lax.optimization_barrier((order, scen_draws))
     copies, table, lines = prepare_call(
         scen_draws,
         factor_mix,
@@ -413,6 +411,8 @@
         holdings.reshape(1, -1),
     )
     own = lax.all_to_all(copies, "far", 0, 0, tiled=True).reshape(-1, copies.shape[2])
+    own, near, core = lax.optimization_barrier((own, near, core))
+    order = ((near + STEPS_Z) % NEAR) * 2 + (core + OTHER) % 2
     half = own.shape[0] // 2
     forward = lambda shocks, place, held: forward_call(
         shocks, place, order, loadings, table, lines, held

time: 188 us -> 188 us (level)
  blocking collectives: 137 us -> 74.2 us
  starting transfers between devices: 12.5 us -> 44.1 us
  waiting for transfers between devices: 2.62 us -> 34.1 us
    all_to_all x1 -> x0, blocking collectives: 63.8 us -> none  [shards(): lax.all_to_all(copies, 'far', 0, 0, tiled=True).reshape(-1, copies.shape[2])]
    all_to_all x0 -> x1, waiting for transfers between devices: none -> 32.2 us  [shards(): lax.all_to_all(copies, 'far', 0, 0, tiled=True).reshape(-1, copies.shape[2])]
    all_to_all x0 -> x1, starting transfers between devices: none -> 31.6 us  [shards(): lax.all_to_all(copies, 'far', 0, 0, tiled=True).reshape(-1, copies.shape[2])]
  transfers between devices with their start and end apart: 9 -> 10, of which waited for: 2 -> 3; matrix products, arithmetic and copies ran while one was open for 0% -> 0% of each run, Pallas kernels for 8% -> 8%
where the time goes in v4:
time: 188 us; the launch traced here: 187 us
  blocking collectives  74.2 us (39%)
  starting transfers between devices  44.1 us (23%)
  waiting for transfers between devices  34.1 us (18%)
  Pallas kernels  30.4 us (16%)
  local copies, waits for them, and re-layouts  2.81 us (1%)
    all_to_all x1, waiting for transfers between devices, shards(): lax.all_to_all(copies, 'far', 0, 0, tiled=True).reshape(-1, copies.shape[2])  32.2 us
    all_to_all x1, starting transfers between devices, shards(): lax.all_to_all(copies, 'far', 0, 0, tiled=True).reshape(-1, copies.shape[2])  31.6 us
    all_to_all x1, blocking collectives, shards(): mine = summed_copies(lax.all_to_all(mine, 'far', 0, 0, tiled=True), CLASSES)  28.4 us
    all_to_all x1, blocking collectives, for_each(): lax.all_to_all(jnp.broadcast_to(x, (lax.axis_size(axis), *x.shape)), axis...  26.8 us
    pallas_call x4, Pallas kernels, forward_call(): pl.pallas_call(lambda *refs: forward_kernel(pieces, first, *refs), grid_s...  17.3 us
    all_to_all x1, blocking collectives, shards(): mine = summed_copies(lax.all_to_all(held[4], CLOSE, 0, 0, tiled=True), FAR)  10.7 us
    pallas_call x1, Pallas kernels, backward_call(): pl.pallas_call(backward_kernel, grid_spec=pltpu.PrefetchScalarGridSpec(nu...  9.72 us
    all_to_all x1, blocking collectives, shards(): sums = lax.all_to_all(mine, CLOSE, 0, 0, tiled=True)  8.32 us
  transfers between devices with their start and end apart: 10, of which 3 were waited for; matrix products, arithmetic and copies ran while one was open for 0% of the time, Pallas kernels for 8%

profile of v4, /device:TPU:38, one launch (start us, length us, event | category | flops | bytes accessed | tf_op | source)
XLA Modules:
  0.0 187.1 jit_solution(5750314938507254039)
XLA Ops:
  0.6 2.2 %prepare.1 = (bf16[8,64,256]{2,1,0:T(8,128)(2,1)}, bf16[128,1024]{1,0:T(8,128)(2,1)}, f32[8,1024]{1,0:T(8,128)}) custom-call(bf16[64,256]{1,0:T(8,128)(2,1)} %refs_0_.1, bf16[256,256]{1,0:T(8,128)(2,1)} %refs_1_.1, s32[1,1024]{1,0:T(1,128)} %bitcast.14, f32[1,128]{1,0:T(1,128)} %bitcast.18, f32[1,1024]{1,0:T(1,128)} %bitcast.15, f32[1,1024]{1,0:T(1,128)} %bitcast.16), custom_call_target="tpu_custom_call" | custom-call | tf_op jit(solution)/shard_map/prepare/pallas_call | solution.py:72
  2.8 31.6 %all-to-all-start = ((bf16[8,64,256]{2,1,0:T(8,128)(2,1)}), bf16[8,64,256]{2,1,0:T(8,128)(2,1)S(1)}, u32[]{:S(2)}, u32[]{:S(2)}) async-start(bf16[8,64,256]{2,1,0:T(8,128)(2,1)} %get-tuple-element.55), calls=%async_computation | async-start | bytes 524288 | tf_op jit(solution)/shard_map/all_to_all | solution.py:413
  34.4 32.2 %all-to-all-done = bf16[8,64,256]{2,1,0:T(8,128)(2,1)S(1)} async-done(((bf16[8,64,256]{2,1,0:T(8,128)(2,1)}), bf16[8,64,256]{2,1,0:T(8,128)(2,1)S(1)}, u32[]{:S(2)}, u32[]{:S(2)}) %all-to-all-start) | async-done | bytes 262176 | tf_op jit(solution)/shard_map/all_to_all | solution.py:413
  66.6 4.5 %collective-permute-start = (bf16[512,256]{1,0:T(8,128)(2,1)S(1)}, bf16[512,256]{1,0:T(8,128)(2,1)S(1)}, u32[]{:S(2)}, u32[]{:S(2)}) collective-permute-start(bf16[512,256]{1,0:T(8,128)(2,1)S(1)} %bitcast.10), channel_id=1, source_target_pairs={{0,62},{2,0},{4,2},{6,4},{8,6},{10,8},{12,10},{14,12},{16,14},{18,... | collective-permute-start | bytes 786440 | tf_op jit(solution)/shard_map/ppermute | solution.py:402
  71.1 4.9 %collective-permute-start.1 = (bf16[512,256]{1,0:T(8,128)(2,1)S(1)}, bf16[512,256]{1,0:T(8,128)(2,1)S(1)}, u32[]{:S(2)}, u32[]{:S(2)}) collective-permute-start(bf16[512,256]{1,0:T(8,128)(2,1)S(1)} %bitcast.11), channel_id=1, source_target_pairs={{0,2},{2,4},{4,6},{6,8},{8,10},{10,12},{12,14},{14,16},{16,18},{18... | collective-permute-start | bytes 786440 | tf_op jit(solution)/shard_map/ppermute | solution.py:403
  76.0 0.7 fusion.refs_0_.order_ref
  76.7 1.0 copy-done
  77.7 0.9 copy-done.1
  78.7 0.8 copy-done.2
  79.5 4.4 %forward_0.1 = (bf16[4096,1024]{1,0:T(8,128)(2,1)S(1)}, bf16[4096,1024]{1,0:T(8,128)(2,1)S(1)}, f32[4096,128]{1,0:T(8,128)S(1)}, bf16[256,4096]{1,0:T(8,128)(2,1)S(1)}, f32[8,8,128]{2,1,0:T(8,128)S(1)}) custom-call(s32[8]{0:T(128)S(1)} %fusion.refs_0_.order_ref, bf16[512,256]{1,0:T(8,128)(2,1)S(1)} %bitcast.12, ...), custom_call_target="tpu_custom_call" | custom-call | flops 805306368 | bytes 4194304 | tf_op jit(solution)/shard_map/forward_0/pallas_call | solution.py:167
  83.8 0.8 collective-permute-done.1.refs_2_
  84.6 0.5 collective-permute-start.6
  85.1 1.9 collective-permute-start.3
  87.3 8.2 %forward_2.1 = (bf16[4096,1024]{1,0:T(8,128)(2,1)S(1)}, bf16[4096,1024]{1,0:T(8,128)(2,1)S(1)}, f32[4096,128]{1,0:T(8,128)S(1)}, bf16[256,4096]{1,0:T(8,128)(2,1)S(1)}, f32[8,8,128]{2,1,0:T(8,128)S(1)}) custom-call(s32[8]{0:T(128)S(1)} %fusion.refs_0_.order_ref, ...), custom_call_target="tpu_custom_call", output_to_operand_aliasing={{0}: (8, {}), {1}: (9, {}), {2}: (10, {}), {3}: (11, {}), {... | custom-call | flops 1610612736 | bytes 8388608 | tf_op jit(solution)/shard_map/forward_2/pallas_call | solution.py:167
  95.5 0.3 collective-permute-start.7
  95.8 2.4 %forward_6.1 = (bf16[4096,1024]{1,0:T(8,128)(2,1)S(1)}, bf16[4096,1024]{1,0:T(8,128)(2,1)S(1)}, f32[4096,128]{1,0:T(8,128)S(1)}, bf16[256,4096]{1,0:T(8,128)(2,1)S(1)}, f32[8,8,128]{2,1,0:T(8,128)S(1)}) custom-call(s32[8]{0:T(128)S(1)} %fusion.refs_0_.order_ref, ...), custom_call_target="tpu_custom_call", output_to_operand_aliasing={{0}: (5, {}), {1}: (6, {}), {2}: (7, {}), {3}: (8, {}), {4}... | custom-call | flops 402653184 | bytes 2097152 | tf_op jit(solution)/shard_map/forward_6/pallas_call | solution.py:167
  98.2 2.4 %forward_7.1 = (bf16[4096,1024]{1,0:T(8,128)(2,1)S(1)}, bf16[4096,1024]{1,0:T(8,128)(2,1)S(1)}, f32[4096,128]{1,0:T(8,128)S(1)}, bf16[256,4096]{1,0:T(8,128)(2,1)S(1)}, f32[8,8,128]{2,1,0:T(8,128)S(1)}) custom-call(s32[8]{0:T(128)S(1)} %fusion.refs_0_.order_ref, ...), custom_call_target="tpu_custom_call", output_to_operand_aliasing={{0}: (5, {}), {1}: (6, {}), {2}: (7, {}), {3}: (8, {}), {4}... | custom-call | flops 402653184 | bytes 2097152 | tf_op jit(solution)/shard_map/forward_7/pallas_call | solution.py:167
  100.6 10.7 %all_to_all.25.x_ref = f32[8,8,128]{2,1,0:T(8,128)S(1)} all-to-all(f32[8,8,128]{2,1,0:T(8,128)S(1)} %get-tuple-element.96), channel_id=1, replica_groups=mesh['groups'=4,'far'=8,'near'=4,'core'=2] {'near','core'}, dimensions={0} | all-to-all | bytes 65536 | tf_op jit(solution)/shard_map/all_to_all | solution.py:435
  111.3 28.4 %all_to_all.26.x_ref = f32[8,8,128]{2,1,0:T(8,128)S(1)} all-to-all(f32[8,8,128]{2,1,0:T(8,128)S(1)} %summed_copies.2), channel_id=1, replica_groups=mesh['groups'=4,'far'=8,'near'=4,'core'=2] {'far'}, dimensions={0} | all-to-all | bytes 65536 | tf_op jit(solution)/shard_map/all_to_all | solution.py:436
  139.7 8.3 %all_to_all.27.refs_0_ = f32[8,8,128]{2,1,0:T(8,128)S(1)} all-to-all(f32[8,8,128]{2,1,0:T(8,128)S(1)} %summed_copies.3), channel_id=1, replica_groups=mesh['groups'=4,'far'=8,'near'=4,'core'=2] {'near','core'}, dimensions={0} | all-to-all | bytes 65536 | tf_op jit(solution)/shard_map/all_to_all | solution.py:437
  148.1 9.7 %backward.1 = (f32[1024,256]{1,0:T(8,128)S(1)}, f32[1,1024]{1,0:T(1,128)S(1)}, f32[1,256]{1,0:T(1,128)S(1)}) custom-call(s32[8]{0:T(128)S(1)} %fusion.refs_0_.order_ref, f32[8,8,128]{2,1,0:T(8,128)S(1)} %all_to_all.27.refs_0_, s32[32,128]{1,0:T(8,128)S(1)} %bitcast.13, bf16[4096,1024]{1,0:T(8,128)(2,1)S(1)} %get-tuple-element.97.refs_2_, ...), custom_call_target="tpu_custom_call" | custom-call | flops 4294967296 | bytes 16777216 | tf_op jit(solution)/shard_map/backward/pallas_call | solution.py:309
  157.9 1.1 collective-permute-done.8
  159.1 26.8 %all_to_all.28.refs_0_ = f32[32,1,256]{2,1,0:T(1,128)S(1)} all-to-all(f32[32,1,256]{2,1,0:T(1,128)S(1)} %broadcast_in_dim.3), channel_id=1, replica_groups=mesh['groups'=4,'far'=8,'near'=4,'core'=2] {'far','near'}, dimensions={0} | all-to-all | bytes 65536 | tf_op jit(solution)/shard_map/all_to_all | solution.py:391
  185.9 1.2 scale.1
  (26 shorter events, 0.6 us)
Async XLA Ops:
  2.8 63.8 %all-to-all-start = ((bf16[8,64,256]{2,1,0:T(8,128)(2,1)}), bf16[8,64,256]{2,1,0:T(8,128)(2,1)S(1)}, u32[]{:S(2)}, u32[]{:S(2)}) async-start(bf16[8,64,256]{2,1,0:T(8,128)(2,1)} %get-tuple-element.55), calls=%async_computation | async-start | bytes 524288 | tf_op jit(solution)/shard_map/all_to_all | solution.py:413
  66.6 10.1 %collective-permute-start.2 = (bf16[512,256]{1,0:T(8,128)(2,1)S(1)}, bf16[512,256]{1,0:T(8,128)(2,1)S(1)}, u32[]{:S(2)}, u32[]{:S(2)}) collective-permute-start(bf16[512,256]{1,0:T(8,128)(2,1)S(1)} %bitcast.9), channel_id=1, source_target_pairs={{0,1},{1,0},{2,3},{3,2},{4,5},{5,4},{6,7},{7,6},{8,9},{9,8},{10,11... | collective-permute-start | bytes 786440 | tf_op jit(solution)/shard_map/ppermute | solution.py:401
  66.6 17.2 %collective-permute-start = (bf16[512,256]{1,0:T(8,128)(2,1)S(1)}, bf16[512,256]{1,0:T(8,128)(2,1)S(1)}, u32[]{:S(2)}, u32[]{:S(2)}) collective-permute-start(bf16[512,256]{1,0:T(8,128)(2,1)S(1)} %bitcast.10), channel_id=1, source_target_pairs={{0,62},{2,0},{4,2},{6,4},{8,6},{10,8},{12,10},{14,12},{16,14},{18,... | collective-permute-start | bytes 786440 | tf_op jit(solution)/shard_map/ppermute | solution.py:402
  71.1 13.5 %collective-permute-start.1 = (bf16[512,256]{1,0:T(8,128)(2,1)S(1)}, bf16[512,256]{1,0:T(8,128)(2,1)S(1)}, u32[]{:S(2)}, u32[]{:S(2)}) collective-permute-start(bf16[512,256]{1,0:T(8,128)(2,1)S(1)} %bitcast.11), channel_id=1, source_target_pairs={{0,2},{2,4},{4,6},{6,8},{8,10},{10,12},{12,14},{14,16},{16,18},{18... | collective-permute-start | bytes 786440 | tf_op jit(solution)/shard_map/ppermute | solution.py:403
  76.7 1.0 copy-start
  77.7 0.9 copy-start.1
  78.7 0.8 copy-start.2
  84.6 2.7 %collective-permute-start.5 = (bf16[512,256]{1,0:T(8,128)(2,1)S(1)}, bf16[512,256]{1,0:T(8,128)(2,1)S(1)}, u32[]{:S(2)}, u32[]{:S(2)}) collective-permute-start(bf16[512,256]{1,0:T(8,128)(2,1)S(1)} %collective-permute-done.refs_1_), channel_id=1, source_target_pairs={{0,1},{1,0},{2,3},{3,2},{4,5},{5,4},{6,7},{7,6},{8,9},{9,8},{10,11... | collective-permute-start | bytes 786440 | tf_op jit(solution)/shard_map/ppermute | solution.py:401
  84.6 2.7 %collective-permute-start.6 = (bf16[512,256]{1,0:T(8,128)(2,1)S(1)}, bf16[512,256]{1,0:T(8,128)(2,1)S(1)}, u32[]{:S(2)}, u32[]{:S(2)}) collective-permute-start(bf16[512,256]{1,0:T(8,128)(2,1)S(1)} %collective-permute-done.1.refs_2_), channel_id=1, source_target_pairs={{0,1},{1,0},{2,3},{3,2},{4,5},{5,4},{6,7},{7,6},{8,9},{9,8},{10,11... | collective-permute-start | bytes 786440 | tf_op jit(solution)/shard_map/ppermute | solution.py:401
  85.1 10.3 %collective-permute-start.3 = (bf16[256,256]{1,0:T(8,128)(2,1)S(1)}, bf16[256,256]{1,0:T(8,128)(2,1)S(1)}, u32[]{:S(2)}, u32[]{:S(2)}) collective-permute-start(bf16[256,256]{1,0:T(8,128)(2,1)S(1)} %slice.6), channel_id=1, source_target_pairs={{0,62},{2,0},{4,2},{6,4},{8,6},{10,8},{12,10},{14,12},{16,14},{18,... | collective-permute-start | bytes 393224 | tf_op jit(solution)/shard_map/ppermute | solution.py:402
  87.0 8.5 %collective-permute-start.4 = (bf16[256,256]{1,0:T(8,128)(2,1)S(1)}, bf16[256,256]{1,0:T(8,128)(2,1)S(1)}, u32[]{:S(2)}, u32[]{:S(2)}) collective-permute-start(bf16[256,256]{1,0:T(8,128)(2,1)S(1)} %slice.7), channel_id=1, source_target_pairs={{0,2},{2,4},{4,6},{6,8},{8,10},{10,12},{12,14},{14,16},{16,18},{18... | collective-permute-start | bytes 393224 | tf_op jit(solution)/shard_map/ppermute | solution.py:403
  95.5 2.7 %collective-permute-start.7 = (bf16[512,256]{1,0:T(8,128)(2,1)S(1)}, bf16[512,256]{1,0:T(8,128)(2,1)S(1)}, u32[]{:S(2)}, u32[]{:S(2)}) collective-permute-start(bf16[512,256]{1,0:T(8,128)(2,1)S(1)} %constant_dynamic-update-slice_fusion.refs_1_), channel_id=1, source_target_pairs={{0,1},{1,0},{2,3},{3,2},{4,5},{5,4},{6,7},{7,6},{8,9},{9,8},{10,11... | collective-permute-start | bytes 786440 | tf_op jit(solution)/shard_map/ppermute | solution.py:401
  98.2 49.8 %copy-start.3 = (f32[8,1024]{1,0:T(8,128)S(1)}, f32[8,1024]{1,0:T(8,128)}, u32[]{:S(2)}) copy-start(f32[8,1024]{1,0:T(8,128)} %get-tuple-element.60.refs_5_.refs_7_.refs_4_.refs_6_) | copy-start | bytes 98308
  98.2 49.8 %copy-start.4 = (s32[4096]{0:T(1024)S(1)}, s32[4096]{0:T(1024)}, u32[]{:S(2)}) copy-start(s32[4096]{0:T(1024)} %param.16) | copy-start | bytes 49156
  157.8 1.3 collective-permute-start.8
